TPU v7x, 256 devices: a whole 4x4x8 slice. The times are simulated.
256 devices in a mesh: rows: 256 (over z, y, x, core).
Axes of the slice: x: 4, y: 4, z: 8, core: 2. Of those that a mesh axis runs over, the one named last changes fastest.
Arguments:
- wave_fn: float32 [512, 3, 3, 512], P('rows')
- left_env: bfloat16 [32, 512, 512], P(None, 'rows')
- op_pair: bfloat16 [32, 9, 9], replicated
- right_env: bfloat16 [32, 512, 512], replicated
Outputs:
- output 1: float32 [7, 512, 3, 3, 512], P(None, 'rows')
- output 2: float32 [6], replicated
- output 3: float32 [6], replicated
All inputs are finite; a program needn't handle non-finite values.
Results may differ from a plain program's by a relative error of at most 0.0127079.
Values are sent between devices in bfloat16 or wider.
A program may use at most 768 MiB of HBM per device.

v0:
```python
import jax
import jax.numpy as jnp
from jax import lax
from jax.sharding import PartitionSpec as P

NUM_STEPS = 6


def solution(mesh):
    row_axis = "rows"

    def local_run(wave_rows, left_rows, op_pair, right_env):
        local_rows = wave_rows.shape[0]
        phys_dim = wave_rows.shape[1]
        bond_dim = wave_rows.shape[3]
        num_terms = left_rows.shape[0]
        pair_dim = phys_dim * phys_dim
        vec_count = bond_dim * bond_dim * pair_dim
        right_flat = jnp.transpose(right_env, (0, 2, 1)).reshape(num_terms * bond_dim, bond_dim)

        def matvec(vec_rows):
            whole_vec = lax.all_gather(vec_rows.astype(jnp.bfloat16), row_axis, axis=0, tiled=True)
            flat_in = whole_vec.reshape(bond_dim, pair_dim * bond_dim)
            left_out = jnp.einsum("kap,pn->kan", left_rows, flat_in, preferred_element_type=jnp.float32)
            left_out = left_out.astype(jnp.bfloat16).reshape(num_terms, local_rows, pair_dim, bond_dim)
            mid_out = jnp.einsum("kqr,karc->aqkc", op_pair, left_out, preferred_element_type=jnp.float32)
            mid_out = mid_out.astype(jnp.bfloat16).reshape(local_rows * pair_dim, num_terms * bond_dim)
            sigma_rows = jnp.dot(mid_out, right_flat, preferred_element_type=jnp.float32)
            return sigma_rows.reshape(local_rows, phys_dim, phys_dim, bond_dim)

        def global_mean(local_val):
            return lax.psum(jnp.sum(local_val), row_axis) / vec_count

        first_vec = wave_rows / jnp.sqrt(global_mean(wave_rows * wave_rows))
        prev_vec = jnp.zeros_like(first_vec)
        cur_vec = first_vec
        beta_prev = jnp.zeros((), jnp.float32)
        vec_list = [first_vec]
        alpha_list = []
        beta_list = []
        for step_idx in range(NUM_STEPS):
            sigma_rows = matvec(cur_vec)
            alpha_val = global_mean(sigma_rows * cur_vec)
            resid_vec = sigma_rows - alpha_val * cur_vec - beta_prev * prev_vec
            beta_val = jnp.sqrt(global_mean(resid_vec * resid_vec))
            next_vec = resid_vec / beta_val
            vec_list.append(next_vec)
            alpha_list.append(alpha_val)
            beta_list.append(beta_val)
            prev_vec = cur_vec
            cur_vec = next_vec
            beta_prev = beta_val
        return jnp.stack(vec_list), jnp.stack(alpha_list), jnp.stack(beta_list)

    return jax.shard_map(local_run, mesh=mesh, in_specs=(P(row_axis), P(None, row_axis), P(), P()), out_specs=(P(None, row_axis), P(), P()), check_vma=False)
```

profile of v0, /device:TPU:1, one launch (start us, length us, event | category | flops | bytes accessed | tf_op | source)
XLA Modules:
  0.0 1832.8 jit_solution(17242820860643131146)
XLA Ops:
  8.6 81.4 %psum.91 = f32[]{:T(128)} all-reduce(f32[]{:T(128)} %multiply_reduce_fusion.12), channel_id=1, replica_groups=mesh['rows'=256] {'rows'}, use_global_device_ids=true, to_apply=%region_1.0 | all-reduce | flops 1 | bytes 8 | tf_op jit(solution)/shard_map/psum | solution.py:32
  93.2 22.6 %copy.79 = bf16[32,512,512]{1,2,0:T(8,128)(2,1)} copy(bf16[32,512,512]{2,1,0:T(8,128)(2,1)} %param.7) | data formatting | bytes 33554432 | tf_op args[3]
  115.7 88.8 %all-gather.7.cloned.1.call-done = bf16[512,3,3,512]{3,2,1,0:T(4,128)(2,1)} async-done(((bf16[2,3,3,512]{3,2,1,0:T(4,128)(2,1)}), bf16[512,3,3,512]{3,2,1,0:T(4,128)(2,1)}) %all-gather.7.cloned.1.call-update) | async-done | bytes 4718608 | tf_op jit(solution)/shard_map/all_gather | solution.py:22
  204.5 10.1 copy.73
  220.1 9.7 multiply_reduce_fusion.11
  229.7 75.0 %psum.92 = f32[]{:T(128)} all-reduce(f32[]{:T(128)} %get-tuple-element.31), channel_id=1, replica_groups=mesh['rows'=256] {'rows'}, use_global_device_ids=true, to_apply=%region_3.0 | all-reduce | flops 1 | bytes 8 | tf_op jit(solution)/shard_map/psum | solution.py:32
  306.0 72.7 %psum.93 = f32[]{:T(128)} all-reduce(f32[]{:T(128)} %multiply_reduce_fusion.10), channel_id=1, replica_groups=mesh['rows'=256] {'rows'}, use_global_device_ids=true, to_apply=%region_5.0 | all-reduce | flops 1 | bytes 8 | tf_op jit(solution)/shard_map/psum | solution.py:32
  380.3 113.1 %all-gather.9.cloned.1.call-done = bf16[512,3,3,512]{3,2,1,0:T(4,128)(2,1)} async-done(((bf16[2,3,3,512]{3,2,1,0:T(4,128)(2,1)}), bf16[512,3,3,512]{3,2,1,0:T(4,128)(2,1)}) %all-gather.9.cloned.1.call-update) | async-done | bytes 4718608 | tf_op jit(solution)/shard_map/all_gather | solution.py:22
  493.4 10.1 copy.81
  508.9 9.7 multiply_reduce_fusion.9
  518.6 75.0 %psum.94 = f32[]{:T(128)} all-reduce(f32[]{:T(128)} %get-tuple-element.33), channel_id=1, replica_groups=mesh['rows'=256] {'rows'}, use_global_device_ids=true, to_apply=%region_7.0 | all-reduce | flops 1 | bytes 8 | tf_op jit(solution)/shard_map/psum | solution.py:32
  594.9 72.7 %psum.95 = f32[]{:T(128)} all-reduce(f32[]{:T(128)} %get-tuple-element.25), channel_id=1, replica_groups=mesh['rows'=256] {'rows'}, use_global_device_ids=true, to_apply=%region_9.0 | all-reduce | flops 1 | bytes 8 | tf_op jit(solution)/shard_map/psum | solution.py:32
  669.2 113.0 %all-gather.11.cloned.1.call-done = bf16[512,3,3,512]{3,2,1,0:T(4,128)(2,1)} async-done(((bf16[2,3,3,512]{3,2,1,0:T(4,128)(2,1)}), bf16[512,3,3,512]{3,2,1,0:T(4,128)(2,1)}) %all-gather.11.cloned.1.call-update) | async-done | bytes 4718608 | tf_op jit(solution)/shard_map/all_gather | solution.py:22
  782.3 10.1 copy.88
  797.8 9.7 multiply_reduce_fusion.7
  807.5 75.0 %psum.96 = f32[]{:T(128)} all-reduce(f32[]{:T(128)} %get-tuple-element.35), channel_id=1, replica_groups=mesh['rows'=256] {'rows'}, use_global_device_ids=true, to_apply=%region_11.0 | all-reduce | flops 1 | bytes 8 | tf_op jit(solution)/shard_map/psum | solution.py:32
  883.8 72.7 %psum.97 = f32[]{:T(128)} all-reduce(f32[]{:T(128)} %get-tuple-element.21), channel_id=1, replica_groups=mesh['rows'=256] {'rows'}, use_global_device_ids=true, to_apply=%region_13.0 | all-reduce | flops 1 | bytes 8 | tf_op jit(solution)/shard_map/psum | solution.py:32
  958.2 113.0 %all-gather.13.cloned.1.call-done = bf16[512,3,3,512]{3,2,1,0:T(4,128)(2,1)} async-done(((bf16[2,3,3,512]{3,2,1,0:T(4,128)(2,1)}), bf16[512,3,3,512]{3,2,1,0:T(4,128)(2,1)}) %all-gather.13.cloned.1.call-update) | async-done | bytes 4718608 | tf_op jit(solution)/shard_map/all_gather | solution.py:22
  1071.2 10.1 copy.95
  1086.7 9.7 multiply_reduce_fusion.5
  1096.4 75.0 %psum.98 = f32[]{:T(128)} all-reduce(f32[]{:T(128)} %get-tuple-element.37), channel_id=1, replica_groups=mesh['rows'=256] {'rows'}, use_global_device_ids=true, to_apply=%region_15.0 | all-reduce | flops 1 | bytes 8 | tf_op jit(solution)/shard_map/psum | solution.py:32
  1172.7 72.7 %psum.99 = f32[]{:T(128)} all-reduce(f32[]{:T(128)} %get-tuple-element.17), channel_id=1, replica_groups=mesh['rows'=256] {'rows'}, use_global_device_ids=true, to_apply=%region_17.0 | all-reduce | flops 1 | bytes 8 | tf_op jit(solution)/shard_map/psum | solution.py:32
  1247.1 113.0 %all-gather.15.cloned.1.call-done = bf16[512,3,3,512]{3,2,1,0:T(4,128)(2,1)} async-done(((bf16[2,3,3,512]{3,2,1,0:T(4,128)(2,1)}), bf16[512,3,3,512]{3,2,1,0:T(4,128)(2,1)}) %all-gather.15.cloned.1.call-update) | async-done | bytes 4718608 | tf_op jit(solution)/shard_map/all_gather | solution.py:22
  1360.0 10.1 copy.102
  1375.6 9.7 multiply_reduce_fusion.3
  1385.3 75.0 %psum.100 = f32[]{:T(128)} all-reduce(f32[]{:T(128)} %get-tuple-element.39), channel_id=1, replica_groups=mesh['rows'=256] {'rows'}, use_global_device_ids=true, to_apply=%region_19.0 | all-reduce | flops 1 | bytes 8 | tf_op jit(solution)/shard_map/psum | solution.py:32
  1461.5 73.1 %psum.101 = f32[]{:T(128)} all-reduce(f32[]{:T(128)} %get-tuple-element.13), channel_id=1, replica_groups=mesh['rows'=256] {'rows'}, use_global_device_ids=true, to_apply=%region_21.0 | all-reduce | flops 1 | bytes 8 | tf_op jit(solution)/shard_map/psum | solution.py:32
  1536.1 113.2 %all-gather.17.cloned.1.call-done = bf16[512,3,3,512]{3,2,1,0:T(4,128)(2,1)} async-done(((bf16[2,3,3,512]{3,2,1,0:T(4,128)(2,1)}), bf16[512,3,3,512]{3,2,1,0:T(4,128)(2,1)}) %all-gather.17.cloned.1.call-update) | async-done | bytes 4718608 | tf_op jit(solution)/shard_map/all_gather | solution.py:22
  1649.3 10.1 copy.109
  1664.8 9.6 multiply_reduce_fusion.1
  1674.5 75.0 %psum.102 = f32[]{:T(128)} all-reduce(f32[]{:T(128)} %get-tuple-element.41), channel_id=1, replica_groups=mesh['rows'=256] {'rows'}, use_global_device_ids=true, to_apply=%region_23.0 | all-reduce | flops 1 | bytes 8 | tf_op jit(solution)/shard_map/psum | solution.py:32
  1750.7 72.7 %psum.103 = f32[]{:T(128)} all-reduce(f32[]{:T(128)} %get-tuple-element.9), channel_id=1, replica_groups=mesh['rows'=256] {'rows'}, use_global_device_ids=true, to_apply=%region_25.0 | all-reduce | flops 1 | bytes 8 | tf_op jit(solution)/shard_map/psum | solution.py:32
  (75 shorter events, 45.8 us)
Async XLA Ops:
  7.2 207.5 %copy-start = (bf16[32,2,512]{2,1,0:T(2,128)(2,1)S(1)}, bf16[32,2,512]{2,1,0:T(2,128)(2,1)}, u32[]{:S(2)}) copy-start(bf16[32,2,512]{2,1,0:T(2,128)(2,1)} %param.5) | copy-start | bytes 196612
  7.2 197.3 %all-gather.7.cloned.1.call-start = ((), (), s32[]{:S(2)}) async-start(), calls=%async_computation | async-start | bytes 6316032 | tf_op jit(solution)/shard_map/all_gather | solution.py:22
  92.1 401.2 %all-gather.9.cloned.1.call-start = ((), (), s32[]{:S(2)}) async-start(), calls=%async_computation.1 | async-start | bytes 6316032 | tf_op jit(solution)/shard_map/all_gather | solution.py:22
  380.1 402.2 %all-gather.11.cloned.1.call-start = ((), (), s32[]{:S(2)}) async-start(), calls=%async_computation.2 | async-start | bytes 6316032 | tf_op jit(solution)/shard_map/all_gather | solution.py:22
  669.0 402.2 %all-gather.13.cloned.1.call-start = ((), (), s32[]{:S(2)}) async-start(), calls=%async_computation.3 | async-start | bytes 6316032 | tf_op jit(solution)/shard_map/all_gather | solution.py:22
  957.9 402.2 %all-gather.15.cloned.1.call-start = ((), (), s32[]{:S(2)}) async-start(), calls=%async_computation.4 | async-start | bytes 6316032 | tf_op jit(solution)/shard_map/all_gather | solution.py:22
  1246.7 402.5 %all-gather.17.cloned.1.call-start = ((), (), s32[]{:S(2)}) async-start(), calls=%async_computation.5 | async-start | bytes 6316032 | tf_op jit(solution)/shard_map/all_gather | solution.py:22
  1824.2 1.2 copy-start.1
Sparse Core Ops, SparseCore 0:
  92.3 112.1 all-gather.6
  380.2 113.1 all-gather.8
  669.1 113.1 all-gather.10
  958.0 113.1 all-gather.12
  1246.9 113.1 all-gather.14
  1536.1 113.1 all-gather.16
where the time goes:
time: 1840 us; the launch traced here: 1830 us
  blocking collectives  968 us (53%)
  waiting for transfers between devices  654 us (36%)
  local copies, waits for them, and re-layouts  96 us (5%)
  matrix products  83.7 us (5%)
  between operations  23.7 us (1%)
    psum x13, blocking collectives, global_mean(): return lax.psum(jnp.sum(local_val), row_axis) / vec_count  968 us
    all_gather x6, waiting for transfers between devices, matvec(): lax.all_gather(vec_rows.astype(jnp.bfloat16), row_axis, axis=0, tiled=True)  654 us
    all_gather x6, local copies, waits for them, and re-layouts, matvec(): lax.all_gather(vec_rows.astype(jnp.bfloat16), row_axis, axis=0, tiled=True)  60.8 us
    dot_general x6, matrix products, matvec(): jnp.dot(mid_out, right_flat, preferred_element_type=jnp.float32)  58.1 us
  transfers between devices with their start and end apart: 6, of which 6 were waited for; matrix products, arithmetic and copies ran while one was open for 1% of the time, Pallas kernels for 0%

commit v1 on v0

v1 whole, which is shorter than its diff:
```python
import functools

import jax
import jax.numpy as jnp
from jax import lax
from jax.experimental import pallas as pl
from jax.experimental.pallas import tpu as pltpu
from jax.sharding import PartitionSpec as P

NUM_STEPS = 6
ROW = "rows"
NY, NX, NC = 4, 4, 2
NS = NY * NX
PAIR = 9
BW = 32
BLK = 72
MESH = pl.DeviceIdType.MESH
F32, BF16 = jnp.float32, jnp.bfloat16
OFFSETS = sorted(
    [(dy, dx) for dy in range(NY) for dx in range(NX) if (dy, dx) != (0, 0)],
    key=lambda o: (-(min(o[0], NY - o[0]) + min(o[1], NX - o[1])), o),
)


def place():
    me = lax.axis_index(ROW)
    return me // (NS * NC), (me // (NX * NC)) % NY, (me // NC) % NX, me % NC


def device(z, y, x, core):
    return ((z * NY + y) * NX + x) * NC + core


def rcopy(src, dst, send_sem, recv_sem, dev):
    return pltpu.make_async_remote_copy(
        src_ref=src, dst_ref=dst, send_sem=send_sem, recv_sem=recv_sem, device_id=(dev,), device_id_type=MESH
    )


def enter(devs):
    barrier = pltpu.get_barrier_semaphore()
    for dev in devs:
        pl.semaphore_signal(barrier, inc=1, device_id=(dev,), device_id_type=MESH)
    pl.semaphore_wait(barrier, len(devs))


def plane_peers(z, y, x, core):
    out = []
    for dy, dx in OFFSETS:
        py, px = (y + dy) % NY, (x + dx) % NX
        out.append((py * NX + px, device(z, py, px, core)))
    return out


def head_kernel(psi_ref, left_ref, psi_out, left_out, p_ss, p_rs, l_ss, l_rs):
    z, y, x, core = place()
    j = y * NX + x
    peers = plane_peers(z, y, x, core)
    enter([dev for _, dev in peers])
    for pj, dev in peers:
        rcopy(psi_ref.at[pj], psi_out.at[j], p_ss.at[pj], p_rs.at[j], dev).start()
    for pj, dev in peers:
        rcopy(left_ref, left_out.at[j], l_ss.at[pj], l_rs.at[j], dev).start()
    psi_out[pl.ds(j, 1)] = psi_ref[pl.ds(j, 1)]
    left_out[pl.ds(j, 1)] = left_ref[...][None]
    for pj, dev in peers:
        rcopy(psi_ref.at[pj], psi_out.at[pj], p_ss.at[pj], p_rs.at[pj], dev).wait()
        rcopy(left_ref, left_out.at[pj], l_ss.at[pj], l_rs.at[pj], dev).wait()


def tail_kernel(vec_ref, vec_out, v_ss, v_rs):
    z, y, x, core = place()
    j = y * NX + x
    peers = plane_peers(z, y, x, core)
    enter([dev for _, dev in peers])
    for pj, dev in peers:
        rcopy(vec_ref.at[pj], vec_out.at[j], v_ss.at[pj], v_rs.at[j], dev).start()
    vec_out[pl.ds(j, 1)] = vec_ref[pl.ds(j, 1)]
    for pj, dev in peers:
        rcopy(vec_ref.at[pj], vec_out.at[pj], v_ss.at[pj], v_rs.at[pj], dev).wait()


def swap4(a, b, c, d):
    lane = lax.broadcasted_iota(jnp.int32, a.shape, 1)
    low = lane < 64
    even = (lane // 32) % 2 == 0
    a, c = jnp.where(low, a, pltpu.roll(c, 64, 1)), jnp.where(low, pltpu.roll(a, 64, 1), c)
    b, d = jnp.where(low, b, pltpu.roll(d, 64, 1)), jnp.where(low, pltpu.roll(b, 64, 1), d)
    a, b = jnp.where(even, a, pltpu.roll(b, 32, 1)), jnp.where(even, pltpu.roll(a, 96, 1), b)
    c, d = jnp.where(even, c, pltpu.roll(d, 32, 1)), jnp.where(even, pltpu.roll(c, 96, 1), d)
    return a, b, c, d


def fold(val):
    return jnp.sum(val.reshape(BLK // 8, 8, 128), axis=0)


def total(val):
    one = jnp.sum(jnp.sum(val, axis=0, keepdims=True), axis=1, keepdims=True)
    return jnp.broadcast_to(one, (1, 128))


def main_kernel(
    nz, count, psi_ref, lt_ref, r2_ref, wv_ref, vout_ref, ab_ref,
    gbuf, vb, ut, xt, y2, sbuf, rbuf, abuf, asend,
    g_ss, d_ss, g_rs, r_ss, r_rs, a_ss, a_rs,
):
    ng = nz * NC
    terms = lt_ref.shape[1] // BW
    z, y, x, core = place()
    i, j = core * nz + z, y * NX + x
    peers = plane_peers(z, y, x, core)
    mate = device(z, y, x, 1 - core)
    zs = [((z + dz) % nz, dz) for dz in sorted(range(1, nz), key=lambda dz: (min(dz, nz - dz), dz))]
    enter([dev for _, dev in peers] + [device(pz, y, x, core) for pz, _ in zs] + [mate])

    vb[...] = jnp.zeros_like(vb)
    gbuf[0, pl.ds(i, 1)] = psi_ref[...][None]

    def gather(par):
        own = gbuf.at[par, i]
        for pz, dz in reversed(zs):
            rcopy(own, own, g_ss.at[dz], g_rs.at[par, i], device(pz, y, x, core)).start()
        rcopy(own, own, g_ss.at[0], g_rs.at[par, i], mate).start()
        for pz, dz in zs:
            slot = core * nz + pz
            ref = gbuf.at[par, slot]
            rcopy(ref, ref, g_ss.at[dz], g_rs.at[par, slot], mate).wait_recv()
            rcopy(ref, ref, d_ss.at[dz], g_rs.at[par, slot], mate).start()
        for dz in range(nz):
            slot = (1 - core) * nz + (z + dz) % nz
            ref = gbuf.at[par, slot]
            rcopy(ref, ref, g_ss.at[0], g_rs.at[par, slot], mate).wait_recv()
        rcopy(own, own, g_ss.at[0], g_rs.at[par, i], mate).wait_send()
        for pz, dz in zs:
            ref = gbuf.at[par, core * nz + pz]
            rcopy(own, own, g_ss.at[dz], g_rs.at[par, i], mate).wait_send()
            rcopy(ref, ref, d_ss.at[dz], g_rs.at[par, i], mate).wait_send()

    def scalars(par, beta_prev):
        zero = jnp.zeros((8, 128), F32)

        def first(s, acc):
            w, v, vp = gbuf[par, s], vb[1 - par, s], vb[par, s]
            return (
                acc[0] + fold(w * v),
                acc[1] + fold((w - beta_prev * vp) * v),
                acc[2] + fold(v * v),
            )

        m, yv, nn = [total(val) for val in lax.fori_loop(0, ng, first, (zero, zero, zero))]
        some = nn > 0.0
        p = jnp.where(some, yv / jnp.where(some, nn, 1.0), 0.0)

        def second(s, acc):
            w, v, vp = gbuf[par, s], vb[1 - par, s], vb[par, s]
            e = w - p * v - beta_prev * vp
            return acc[0] + fold(e * e), acc[1] + fold(e * v)

        ee, ev = [total(val) for val in lax.fori_loop(0, ng, second, (zero, zero))]
        row = lax.broadcasted_iota(jnp.int32, (8, 128), 0)
        tile = jnp.where(row == 0, m, jnp.where(row == 1, p, jnp.where(row == 2, nn, jnp.where(row == 3, ee, ev))))
        asend[...] = tile
        for pj, dev in peers:
            rcopy(asend, abuf.at[j], a_ss.at[pj], a_rs.at[j], dev).start()
        abuf[pl.ds(j, 1)] = tile[None]
        for pj, dev in peers:
            rcopy(asend, abuf.at[pj], a_ss.at[pj], a_rs.at[pj], dev).wait()
        alpha = abuf[0, 0:1]
        for s in range(1, NS):
            alpha = alpha + abuf[s, 0:1]
        alpha = alpha / count
        square = jnp.zeros((1, 128), F32)
        for s in range(NS):
            off = abuf[s, 1:2] - alpha
            square = square + (abuf[s, 3:4] + 2.0 * (off * abuf[s, 4:5]) + (off * abuf[s, 2:3]) * off)
        return alpha, jnp.sqrt(square / count)

    def left_and_mix(par):
        for grp in range(ng // 4):
            lanes = slice(grp * 128, grp * 128 + 128)
            for t in range(2):
                outs = swap4(*[vb[par, grp * 4 + ii, t * 32 : t * 32 + 32] for ii in range(4)])
                for k in range(4):
                    q = 4 * t + k
                    ut[q * 32 : q * 32 + 32, lanes] = outs[k].astype(BF16)
            outs = swap4(*[vb[par, grp * 4 + ii, 64:72] for ii in range(4)])
            ut[256:272, lanes] = jnp.concatenate(outs[:2], axis=0).astype(BF16)
            ut[272:288, lanes] = jnp.concatenate(outs[2:], axis=0).astype(BF16)
        width = 256
        for part in range(terms * BW // width):
            cols = slice(part * width, part * width + width)
            xt[:, cols] = jnp.dot(ut[...], lt_ref[:, cols], preferred_element_type=F32)

        def mix(grp, carry):
            lanes = pl.ds(pl.multiple_of(grp * 128, 128), 128)
            xs = [xt[r * 32 : r * 32 + 32, lanes].astype(BF16).astype(F32) for r in range(PAIR)]

            def one(q):
                acc = wv_ref[q * PAIR : q * PAIR + 1, lanes] * xs[0]
                for r in range(1, PAIR):
                    acc = acc + wv_ref[q * PAIR + r : q * PAIR + r + 1, lanes] * xs[r]
                return acc

            rows = [pl.ds(pl.multiple_of(grp * 128 + k * 32, 32), 32) for k in range(4)]
            for t in range(2):
                outs = swap4(*[one(4 * t + k) for k in range(4)])
                for k in range(4):
                    y2[rows[k], t * 128 : t * 128 + 128] = outs[k].astype(BF16)
            last = one(8)
            for k in range(4):
                moved = last if k == 0 else pltpu.roll(last, 128 - 32 * k, 1)
                y2[rows[k], 256:384] = moved.astype(BF16)
            return carry

        lax.fori_loop(0, terms * BW // 128, mix, 0)

    def right_and_scatter(nxt):
        grp = lax.broadcasted_iota(jnp.int32, (8, 128), 1) // 32
        for dy in (2, 1, 3, 0):
            py = (y + dy) % NY
            part = jnp.dot(
                r2_ref[pl.ds(pl.multiple_of(py * 128, 128), 128), :], y2[...], preferred_element_type=F32
            )
            for px in range(NX):
                pj = py * NX + px
                rows = part[px * 32 : px * 32 + 32]
                packed = rows[0:8, 256:384]
                for t in range(1, 4):
                    packed = jnp.where(grp == t, pltpu.roll(rows[8 * t : 8 * t + 8, 256:384], 32 * t, 1), packed)
                sbuf[pj, 0:32] = rows[:, 0:128]
                sbuf[pj, 32:64] = rows[:, 128:256]
                sbuf[pj, 64:72] = packed
                send = rcopy(sbuf.at[pj], rbuf.at[j], r_ss.at[pj], r_rs.at[j], device(z, py, px, core))
                if dy:
                    send.start()
                else:

                    @pl.when(px != x)
                    def _():
                        send.start()

        rbuf[pl.ds(j, 1)] = sbuf[pl.ds(j, 1)]
        for pj, dev in reversed(peers):
            rcopy(sbuf.at[pj], rbuf.at[pj], r_ss.at[pj], r_rs.at[pj], dev).wait()
        w = rbuf[0]
        for s in range(1, NS):
            w = w + rbuf[s]
        gbuf[nxt, pl.ds(i, 1)] = w[None]

    def step(t, beta_prev):
        par = t % 2
        gather(par)
        alpha, beta = scalars(par, beta_prev)
        ab_ref[0, pl.ds(t, 1)] = alpha
        ab_ref[1, pl.ds(t, 1)] = beta

        def update(s, carry):
            w, v, vp = gbuf[par, s], vb[1 - par, s], vb[par, s]
            vb[par, pl.ds(s, 1)] = ((w - alpha * v - beta_prev * vp) / beta)[None]
            return carry

        lax.fori_loop(0, ng, update, 0)
        vout_ref[pl.ds(t, 1)] = vb[par, pl.ds(i, 1)]

        @pl.when(t < NUM_STEPS)
        def _():
            left_and_mix(par)
            right_and_scatter(1 - par)

        return jnp.where(t == 0, jnp.zeros_like(beta), beta)

    lax.fori_loop(0, NUM_STEPS + 1, step, jnp.zeros((1, 128), F32))


def vmem(n):
    return [pl.BlockSpec(memory_space=pltpu.VMEM)] * n


def dma(*shape):
    return pltpu.SemaphoreType.DMA(shape)


def solution(mesh):
    nz = mesh.shape[ROW] // (NS * NC)
    ng = nz * NC

    def local_run(wave_rows, left_rows, op_pair, right_env):
        terms, rows, left_dim = left_rows.shape
        right_dim = right_env.shape[1]
        count = left_dim * right_dim * PAIR
        j = (lax.axis_index(ROW) // NC) % NS

        psi = wave_rows.reshape(rows, PAIR, NS, BW).transpose(2, 0, 1, 3).reshape(NS, rows * PAIR * BW)
        psi = jnp.pad(psi, ((0, 0), (0, 1024 - psi.shape[1]))).reshape(NS, 8, 128)
        left = left_rows.reshape(terms, rows, nz, NS, NC, rows).transpose(0, 1, 4, 2, 3, 5).reshape(terms * rows, left_dim)
        psi, left = pl.pallas_call(
            head_kernel,
            out_shape=(jax.ShapeDtypeStruct((NS, 8, 128), F32), jax.ShapeDtypeStruct((NS, terms * rows, left_dim), BF16)),
            in_specs=vmem(2),
            out_specs=tuple(vmem(2)),
            scratch_shapes=[dma(NS), dma(NS), dma(NS), dma(NS)],
            compiler_params=pltpu.CompilerParams(collective_id=0, has_side_effects=True),
            name="head",
        )(psi, left)
        psi = psi.reshape(NS, 1024)[:, : rows * PAIR * BW].reshape(NS, rows, PAIR, BW)
        psi = psi.transpose(2, 3, 0, 1).reshape(PAIR, BW, BW)
        main = psi[:8].reshape(2, 4, BW, BW).transpose(0, 2, 1, 3).reshape(64, 128)
        last = psi[8].reshape(4, 8, BW).transpose(1, 0, 2).reshape(8, 128)
        psi = jnp.concatenate([main, last], axis=0)
        lt = left.reshape(NS, terms, rows, left_dim).transpose(3, 1, 0, 2).reshape(left_dim, terms * BW)
        r2 = lax.dynamic_slice_in_dim(right_env, j * BW, BW, axis=1)
        r2 = r2.transpose(2, 0, 1).reshape(right_dim, terms * BW)
        wv = jnp.repeat(op_pair.astype(F32).transpose(1, 2, 0).reshape(PAIR * PAIR, terms), BW, axis=1)

        vblk, ab = pl.pallas_call(
            functools.partial(main_kernel, nz, float(count)),
            out_shape=(jax.ShapeDtypeStruct((NUM_STEPS + 1, BLK, 128), F32), jax.ShapeDtypeStruct((2, 8, 128), F32)),
            in_specs=vmem(4),
            out_specs=tuple(vmem(2)),
            scratch_shapes=[
                pltpu.VMEM((2, ng, BLK, 128), F32),
                pltpu.VMEM((2, ng, BLK, 128), F32),
                pltpu.VMEM((PAIR * BW, left_dim), BF16),
                pltpu.VMEM((PAIR * BW, terms * BW), F32),
                pltpu.VMEM((terms * BW, 384), BF16),
                pltpu.VMEM((NS, BLK, 128), F32),
                pltpu.VMEM((NS, BLK, 128), F32),
                pltpu.VMEM((NS, 8, 128), F32),
                pltpu.VMEM((8, 128), F32),
                dma(nz), dma(nz), dma(2, ng), dma(NS), dma(NS), dma(NS), dma(NS),
            ],
            compiler_params=pltpu.CompilerParams(
                collective_id=1, has_side_effects=True, vmem_limit_bytes=48 * 1024 * 1024
            ),
            name="lanczos",
        )(psi, lt, r2, wv)

        nv = NUM_STEPS + 1
        main = vblk[:, :64].reshape(nv, 2, BW, 4, NS, rows).transpose(4, 0, 5, 1, 3, 2).reshape(NS, nv, rows, 8, BW)
        last = vblk[:, 64:].reshape(nv, 8, 4, NS, rows).transpose(3, 0, 4, 2, 1).reshape(NS, nv, rows, 1, BW)
        vecs = jnp.concatenate([main, last], axis=3).reshape(NS, nv * rows * PAIR * BW)
        vecs = jnp.pad(vecs, ((0, 0), (0, 4096 - vecs.shape[1]))).reshape(NS, 32, 128)
        vecs = pl.pallas_call(
            tail_kernel,
            out_shape=jax.ShapeDtypeStruct((NS, 32, 128), F32),
            in_specs=vmem(1),
            out_specs=vmem(1)[0],
            scratch_shapes=[dma(NS), dma(NS)],
            compiler_params=pltpu.CompilerParams(collective_id=2, has_side_effects=True),
            name="tail",
        )(vecs)
        vecs = vecs.reshape(NS, 4096)[:, : nv * rows * PAIR * BW].reshape(NS, nv, rows, PAIR, BW)
        vecs = vecs.transpose(1, 2, 3, 0, 4).reshape(nv, rows, 3, 3, right_dim)
        return vecs, ab[0, 1 : NUM_STEPS + 1, 0], ab[1, 1 : NUM_STEPS + 1, 0]

    return jax.shard_map(
        local_run,
        mesh=mesh,
        in_specs=(P(ROW), P(None, ROW), P(), P()),
        out_specs=(P(None, ROW), P(), P()),
        check_vma=False,
    )
```

time: 1840 us -> 260 us (0.14)
  blocking collectives: 968 us -> 0 us
  waiting for transfers between devices: 654 us -> 0 us
  Pallas kernels: 0 us -> 226 us
  matrix products: 83.7 us -> 0 us
  local copies, waits for them, and re-layouts: 96 us -> 33 us
  between operations: 23.7 us -> 0.95 us
    psum x13 -> x0, blocking collectives: 968 us -> none  [global_mean(): return lax.psum(jnp.sum(local_val), row_axis) / vec_count]
    all_gather x6 -> x0, waiting for transfers between devices: 654 us -> none  [matvec(): lax.all_gather(vec_rows.astype(jnp.bfloat16), row_axis, axis=0, tiled=True)]
    pallas_call x0 -> x3, Pallas kernels: none -> 226 us  [the longest x1 191 us: local_run(): pl.pallas_call(functools.partial(main_kernel, nz, float(count)), out_shap...]
    dot_general x18 -> x0, matrix products: 83.7 us -> none  [the longest x6 58.1 us: matvec(): jnp.dot(mid_out, right_flat, preferred_element_type=jnp.float32)]
    all_gather x6 -> x0, local copies, waits for them, and re-layouts: 60.8 us -> none  [matvec(): lax.all_gather(vec_rows.astype(jnp.bfloat16), row_axis, axis=0, tiled=True)]
    unnamed x12 -> x9, local copies, waits for them, and re-layouts: 23.6 us -> 4.4 us
  transfers between devices with their start and end apart: 6 -> 0, of which waited for: 6 -> 0; matrix products, arithmetic and copies ran while one was open for 1% -> 0% of each run, Pallas kernels for 0% -> 0%
where the time goes in v1:
time: 260 us
  Pallas kernels  226 us (87%)
  local copies, waits for them, and re-layouts  33 us (13%)
    pallas_call x1, Pallas kernels, local_run(): pl.pallas_call(functools.partial(main_kernel, nz, float(count)), out_shap...  191 us
    pallas_call x1, Pallas kernels, local_run(): pl.pallas_call(head_kernel, out_shape=(jax.ShapeDtypeStruct((NS, 8, 128),...  24 us
    pallas_call x1, Pallas kernels, local_run(): pl.pallas_call(tail_kernel, out_shape=jax.ShapeDtypeStruct((NS, 32, 128),...  11.2 us
    transpose x1, local copies, waits for them, and re-layouts, local_run(): left_rows.reshape(terms, rows, nz, NS, NC, rows).transpose(0, 1, 4, 2, 3, 5)  8.02 us
    reshape x1, local copies, waits for them, and re-layouts, local_run(): left_rows.reshape(terms, rows, nz, NS, NC, rows).transpose(0, 1, 4, 2, 3, 5)  7.79 us

profile of v1, /device:TPU:1, one launch (start us, length us, event | category | flops | bytes accessed | tf_op | source)
XLA Modules:
  0.0 260.1 jit_solution(9107427633799214845)
XLA Ops:
  0.6 0.9 reshape.86
  1.6 0.1 reshape.87
  1.7 0.6 copy.47
  2.4 1.0 copy.30
  3.4 8.0 %copy.31 = bf16[32,2,2,8,16,2]{5,4,3,2,1,0:T(8,128)(2,1)} copy(bf16[32,2,2,8,16,2]{0,5,2,4,3,1:T(2,128)(2,1)S(1)} %bitcast.63) | data formatting | bytes 131072 | tf_op jit(solution)/shard_map/transpose | solution.py:296
  11.4 7.8 %reshape.90.left_ref = bf16[64,512]{1,0:T(8,128)(2,1)} reshape(bf16[32,2,2,8,16,2]{5,4,3,2,1,0:T(8,128)(2,1)} %copy.31) | data formatting | bytes 131072 | tf_op jit(solution)/shard_map/reshape | solution.py:296
  19.2 24.0 %head.1 = (f32[16,8,128]{2,1,0:T(8,128)}, bf16[16,64,512]{2,1,0:T(8,128)(2,1)}) custom-call(f32[16,8,128]{2,1,0:T(8,128)} %bitcast.73, bf16[64,512]{1,0:T(8,128)(2,1)} %reshape.90.left_ref), custom_call_target="tpu_custom_call" | custom-call | tf_op jit(solution)/shard_map/head/pallas_call | solution.py:297
  43.3 0.9 copy.58
  44.8 0.1 reshape.94
  44.9 1.5 reshape.96
  46.4 1.1 copy.55
  47.5 0.4 reshape.97
  47.9 0.5 copy.37.lt_ref
  48.5 1.3 constant_dynamic-slice_fusion
  49.9 0.5 copy.38.r2_ref
  50.6 0.2 copy.39.wv_ref
  50.8 190.7 %lanczos.1 = (f32[7,72,128]{2,1,0:T(8,128)S(1)}, f32[2,8,128]{2,1,0:T(8,128)S(1)}) custom-call(f32[72,128]{1,0:T(8,128)S(1)} %pad_maximum_fusion.1.psi_ref, bf16[512,1024]{1,0:T(8,128)(2,1)S(1)} %copy.37.lt_ref, bf16[512,1024]{1,0:T(8,128)(2,1)S(1)} %copy.38.r2_ref, f32[81,1024]{1,0:T(8,128)S(1)} %copy.39.wv_ref), custom_call_target="tpu_custom_call" | custom-call | tf_op jit(solution)/shard_map/lanczos/pallas_call | solution.py:316
  241.5 0.2 copy.42
  241.7 0.2 copy.43
  241.9 0.1 copy.44
  242.0 0.2 copy.40
  242.2 0.5 reshape.102
  242.8 0.1 copy.41
  243.0 0.4 copy.45
  243.4 0.5 reshape.106
  243.9 0.7 copy.49
  244.7 11.2 %tail.1 = f32[16,32,128]{2,1,0:T(8,128)} custom-call(f32[16,32,128]{2,1,0:T(8,128)} %bitcast.65), custom_call_target="tpu_custom_call" | custom-call | tf_op jit(solution)/shard_map/tail/pallas_call | solution.py:344
  255.9 1.1 copy.56
  257.0 0.6 reshape.109
  257.6 0.6 copy.46
  258.2 1.2 reshape.110
  259.4 0.7 slice_reduce_fusion.1
  (22 shorter events, 1.0 us)
Async XLA Ops:
  47.5 2.9 %copy-start = (bf16[32,9,9]{0,2,1:T(8,128)(2,1)S(1)}, bf16[32,9,9]{0,2,1:T(8,128)(2,1)}, u32[]{:S(2)}) copy-start(bf16[32,9,9]{0,2,1:T(8,128)(2,1)} %param.6) | copy-start | bytes 15556

commit v2 on v1

v2 whole, which is shorter than its diff:
```python
import functools

import jax
import jax.numpy as jnp
from jax import lax
from jax.experimental import pallas as pl
from jax.experimental.pallas import tpu as pltpu
from jax.sharding import PartitionSpec as P

NUM_STEPS = 6
ROW = "rows"
NY, NX, NC = 4, 4, 2
NS = NY * NX
PAIR = 9
BW = 32
BLK = 72
MESH = pl.DeviceIdType.MESH
F32, BF16 = jnp.float32, jnp.bfloat16
OFFSETS = sorted(
    [(dy, dx) for dy in range(NY) for dx in range(NX) if (dy, dx) != (0, 0)],
    key=lambda o: (-(min(o[0], NY - o[0]) + min(o[1], NX - o[1])), o),
)


def place():
    me = lax.axis_index(ROW)
    return me // (NS * NC), (me // (NX * NC)) % NY, (me // NC) % NX, me % NC


def device(z, y, x, core):
    return ((z * NY + y) * NX + x) * NC + core


def rcopy(src, dst, send_sem, recv_sem, dev):
    return pltpu.make_async_remote_copy(
        src_ref=src, dst_ref=dst, send_sem=send_sem, recv_sem=recv_sem, device_id=(dev,), device_id_type=MESH
    )


def enter(devs):
    barrier = pltpu.get_barrier_semaphore()
    for dev in devs:
        pl.semaphore_signal(barrier, inc=1, device_id=(dev,), device_id_type=MESH)
    pl.semaphore_wait(barrier, len(devs))


def plane_peers(z, y, x, core):
    out = []
    for dy, dx in OFFSETS:
        py, px = (y + dy) % NY, (x + dx) % NX
        out.append((py * NX + px, device(z, py, px, core)))
    return out


def swap4(a, b, c, d):
    lane = lax.broadcasted_iota(jnp.int32, a.shape, 1)
    low = lane < 64
    even = (lane // 32) % 2 == 0
    a, c = jnp.where(low, a, pltpu.roll(c, 64, 1)), jnp.where(low, pltpu.roll(a, 64, 1), c)
    b, d = jnp.where(low, b, pltpu.roll(d, 64, 1)), jnp.where(low, pltpu.roll(b, 64, 1), d)
    a, b = jnp.where(even, a, pltpu.roll(b, 32, 1)), jnp.where(even, pltpu.roll(a, 96, 1), b)
    c, d = jnp.where(even, c, pltpu.roll(d, 32, 1)), jnp.where(even, pltpu.roll(c, 96, 1), d)
    return a, b, c, d


def fold(val):
    return jnp.sum(val.reshape(BLK // 8, 8, 128), axis=0)


def total(val):
    one = jnp.sum(jnp.sum(val, axis=0, keepdims=True), axis=1, keepdims=True)
    return jnp.broadcast_to(one, (1, 128))


def block(main, last):
    return jnp.concatenate([main[0], main[1], last], axis=0)


def pack_last(rows):
    grp = lax.broadcasted_iota(jnp.int32, (8, 128), 1) // 32
    packed = rows[0:8]
    for t in range(1, 4):
        packed = jnp.where(grp == t, pltpu.roll(rows[8 * t : 8 * t + 8], 32 * t, 1), packed)
    return packed


def unpack_last(tile):
    return jnp.concatenate([tile if t == 0 else pltpu.roll(tile, 128 - 32 * t, 1) for t in range(4)], axis=0)


def rows5(vals):
    row = lax.broadcasted_iota(jnp.int32, (8, 128), 0)
    tile = vals[4]
    for k in (3, 2, 1, 0):
        tile = jnp.where(row == k, vals[k], tile)
    return jnp.broadcast_to(tile, (8, 128))


def ratio(num, den):
    some = den > 0.0
    return jnp.where(some, num / jnp.where(some, den, 1.0), 0.0)


def main_kernel(
    nz, count, psi_ref, left_ref, op_ref, right_ref, vec_ref, alpha_ref, beta_ref,
    gbuf, vb, ut, xt, y2, sbuf, rbuf, abuf, asend, cbuf, lt, r2, wv, lf, lsend, lrecv, rt, psend, precv, osend, orecv, mt,
    g_ss, d_ss, g_rs, r_ss, r_rs, a_ss, a_rs, c_ss, c_rs, l_ss, l_rs, p_ss, p_rs, o_ss, o_rs, rt_sem,
):
    ng = nz * NC
    terms = left_ref.shape[0]
    left_dim = left_ref.shape[2]
    z, y, x, core = place()
    i, j = core * nz + z, y * NX + x
    peers = plane_peers(z, y, x, core)
    mate = device(z, y, x, 1 - core)
    zs = [((z + dz) % nz, dz) for dz in sorted(range(1, nz), key=lambda dz: (min(dz, nz - dz), dz))]
    line = [(core, pz, dz) for pz, dz in zs] + [(1 - core, pz, nz + dz) for pz, dz in zs] + [(1 - core, z, nz)]

    load_right = pltpu.make_async_copy(right_ref.at[:, pl.ds(pl.multiple_of(j * BW, BW), BW), :], rt, rt_sem)
    load_right.start()
    enter([dev for _, dev in peers] + [device(pz, y, x, pc) for pc, pz, _ in line])

    def start_gather(par):
        own = gbuf.at[par, i]
        for pz, dz in reversed(zs):
            rcopy(own, own, g_ss.at[dz], g_rs.at[par, i], device(pz, y, x, core)).start()
        rcopy(own, own, g_ss.at[0], g_rs.at[par, i], mate).start()

    def relay(par, some):
        for pz, dz in some:
            slot = core * nz + pz
            ref = gbuf.at[par, slot]
            rcopy(ref, ref, g_ss.at[dz], g_rs.at[par, slot], mate).wait_recv()
            rcopy(ref, ref, d_ss.at[dz], g_rs.at[par, slot], mate).start()

    def finish_gather(par):
        for dz in range(nz):
            slot = (1 - core) * nz + (z + dz) % nz
            ref = gbuf.at[par, slot]
            rcopy(ref, ref, g_ss.at[0], g_rs.at[par, slot], mate).wait_recv()
        own = gbuf.at[par, i]
        rcopy(own, own, g_ss.at[0], g_rs.at[par, i], mate).wait_send()
        for pz, dz in zs:
            ref = gbuf.at[par, core * nz + pz]
            rcopy(own, own, g_ss.at[dz], g_rs.at[par, i], mate).wait_send()
            rcopy(ref, ref, d_ss.at[dz], g_rs.at[par, i], mate).wait_send()

    def start_line(par, vals):
        cbuf[par, pl.ds(i, 1)] = rows5(vals)[None]
        own = cbuf.at[par, i]
        for pc, pz, k in line:
            rcopy(own, own, c_ss.at[k], c_rs.at[par, i], device(pz, y, x, pc)).start()

    def finish_line(par):
        own = cbuf.at[par, i]
        for pc, pz, k in line:
            slot = pc * nz + pz
            rcopy(own, cbuf.at[par, slot], c_ss.at[k], c_rs.at[par, slot], mate).wait()
        alpha = cbuf[par, 0, 0:1]
        for s in range(1, ng):
            alpha = alpha + cbuf[par, s, 0:1]
        alpha = alpha / count
        square = jnp.zeros((1, 128), F32)
        for s in range(ng):
            off = cbuf[par, s, 1:2] - alpha
            square = square + (cbuf[par, s, 3:4] + 2.0 * (off * cbuf[par, s, 4:5]) + (off * cbuf[par, s, 2:3]) * off)
        return alpha, jnp.sqrt(square / count)

    def start_plane(par, beta_prev):
        w, v, vp = gbuf[par, i], vb[1 - par, i], vb[par, i]
        rest = w - beta_prev * vp
        m, yv, nn = total(fold(w * v)), total(fold(rest * v)), total(fold(v * v))
        p = ratio(yv, nn)
        e = rest - p * v
        tile = rows5([m, p, nn, total(fold(e * e)), total(fold(e * v))])
        asend[...] = tile
        for pj, dev in peers:
            rcopy(asend, abuf.at[j], a_ss.at[pj], a_rs.at[j], dev).start()
        abuf[pl.ds(j, 1)] = tile[None]

    def finish_plane():
        for pj, dev in peers:
            rcopy(asend, abuf.at[pj], a_ss.at[pj], a_rs.at[pj], dev).wait()
        zero = jnp.zeros((1, 128), F32)
        m, nn, pn, ee, ev = zero, zero, zero, zero, zero
        for s in range(NS):
            m, nn, pn = m + abuf[s, 0:1], nn + abuf[s, 2:3], pn + abuf[s, 1:2] * abuf[s, 2:3]
        p = ratio(pn, nn)
        for s in range(NS):
            off = abuf[s, 1:2] - p
            ee = ee + (abuf[s, 3:4] + 2.0 * (off * abuf[s, 4:5]) + (off * abuf[s, 2:3]) * off)
            ev = ev + (abuf[s, 4:5] + off * abuf[s, 2:3])
        return [m, p, nn, ee, ev]

    early, final = (osend, orecv, o_ss, o_rs), (psend, precv, p_ss, p_rs)

    def start_out(par, bufs):
        send, recv, ss, rs = bufs
        blk = vb[par, i]
        last = unpack_last(blk[64:72])
        mt[...] = jnp.concatenate([blk[:64], last, jnp.zeros((32, 128), F32)], axis=0).T
        for pj in range(NS):
            for k in range(4):
                send[pj, 2 * k : 2 * k + 2] = mt[k * 32 + 2 * pj : k * 32 + 2 * pj + 2]
        for pj, dev in peers:
            rcopy(send.at[pj], recv.at[j], ss.at[pj], rs.at[j], dev).start()
        recv[pl.ds(j, 1)] = send[pl.ds(j, 1)]

    def finish_out(num, bufs):
        send, recv, ss, rs = bufs
        for pj, dev in peers:
            rcopy(send.at[pj], recv.at[pj], ss.at[pj], rs.at[pj], dev).wait()
        for grp in range(NS // 4):
            outs = swap4(*[recv[grp * 4 + k] for k in range(4)])
            lanes = slice(grp * 128, grp * 128 + 128)
            for t in range(2):
                for k in range(4):
                    vec_ref[num, 4 * t + k, :, lanes] = outs[t][2 * k : 2 * k + 2]
            vec_ref[num, 8, :, lanes] = outs[2][0:2]

    def update(par, alpha, beta_prev, beta, first, size):
        def body(s, carry):
            w, v, vp = gbuf[par, s], vb[1 - par, s], vb[par, s]
            vb[par, pl.ds(s, 1)] = ((w - alpha * v - beta_prev * vp) / beta)[None]
            return carry

        lax.fori_loop(first, first + size, body, 0)

    def left_and_mix(par):
        for grp in range(ng // 4):
            lanes = slice(grp * 128, grp * 128 + 128)
            for t in range(2):
                outs = swap4(*[vb[par, grp * 4 + ii, t * 32 : t * 32 + 32] for ii in range(4)])
                for k in range(4):
                    q = 4 * t + k
                    ut[q * 32 : q * 32 + 32, lanes] = outs[k].astype(BF16)
            outs = swap4(*[vb[par, grp * 4 + ii, 64:72] for ii in range(4)])
            ut[256:272, lanes] = jnp.concatenate(outs[:2], axis=0).astype(BF16)
            ut[272:288, lanes] = jnp.concatenate(outs[2:], axis=0).astype(BF16)
        width = 256
        for part in range(terms * BW // width):
            cols = slice(part * width, part * width + width)
            xt[:, cols] = jnp.dot(ut[...], lt[:, cols], preferred_element_type=F32)

        def mix(grp, carry):
            lanes = pl.ds(pl.multiple_of(grp * 128, 128), 128)
            xs = [xt[r * 32 : r * 32 + 32, lanes].astype(BF16).astype(F32) for r in range(PAIR)]

            def one(q):
                acc = wv[q * 16 : q * 16 + 1, lanes] * xs[0]
                for r in range(1, PAIR):
                    acc = acc + wv[q * 16 + r : q * 16 + r + 1, lanes] * xs[r]
                return acc

            rows = [pl.ds(pl.multiple_of(grp * 128 + k * 32, 32), 32) for k in range(4)]
            for t in range(2):
                outs = swap4(*[one(4 * t + k) for k in range(4)])
                for k in range(4):
                    y2[rows[k], t * 128 : t * 128 + 128] = outs[k].astype(BF16)
            last = one(8)
            for k in range(4):
                moved = last if k == 0 else pltpu.roll(last, 128 - 32 * k, 1)
                y2[rows[k], 256:384] = moved.astype(BF16)
            return carry

        lax.fori_loop(0, terms * BW // 128, mix, 0)

    def right_and_scatter(nxt):
        for dy in (2, 1, 3, 0):
            py = (y + dy) % NY
            part = jnp.dot(
                r2[pl.ds(pl.multiple_of(py * 128, 128), 128), :], y2[...], preferred_element_type=F32
            )
            for px in range(NX):
                pj = py * NX + px
                rows = part[px * 32 : px * 32 + 32]
                sbuf[pj, 0:32] = rows[:, 0:128]
                sbuf[pj, 32:64] = rows[:, 128:256]
                sbuf[pj, 64:72] = pack_last(rows[:, 256:384])
                send = rcopy(sbuf.at[pj], rbuf.at[j], r_ss.at[pj], r_rs.at[j], device(z, py, px, core))
                if dy:
                    send.start()
                else:

                    @pl.when(px != x)
                    def _():
                        send.start()

        rbuf[pl.ds(j, 1)] = sbuf[pl.ds(j, 1)]
        for pj, dev in reversed(peers):
            rcopy(sbuf.at[pj], rbuf.at[pj], r_ss.at[pj], r_rs.at[pj], dev).wait()
        w = rbuf[0]
        for s in range(1, NS):
            w = w + rbuf[s]
        gbuf[nxt, pl.ds(i, 1)] = w[None]

    norm = jnp.zeros((1, 128), F32)
    for grp in range(NS // 4):
        lanes = slice(grp * 128, grp * 128 + 128)
        for q in range(PAIR):
            norm = norm + jnp.sum(psi_ref[q, :, lanes] * psi_ref[q, :, lanes], axis=0, keepdims=True)
    norm = jnp.broadcast_to(jnp.sum(norm, axis=1, keepdims=True), (8, 128))
    for t in range(3):
        mt[8 * t : 8 * t + 8] = jnp.zeros((8, 128), F32)
    for grp in range(NS // 4):
        lanes = slice(grp * 128, grp * 128 + 128)
        for q in range(PAIR):
            mt[2 * q : 2 * q + 2] = psi_ref[q, :, lanes]
        outs = swap4(mt[0:8], mt[8:16], mt[16:24], norm)
        for k in range(4):
            psend[grp * 4 + k] = outs[k]
    for pj, dev in peers:
        rcopy(psend.at[pj], precv.at[j], p_ss.at[pj], p_rs.at[j], dev).start()
    precv[pl.ds(j, 1)] = psend[pl.ds(j, 1)]

    for k in range(terms):
        lf[2 * k : 2 * k + 2] = left_ref[k].astype(F32)
    row = lax.broadcasted_iota(jnp.int32, (left_dim, left_dim), 0)
    col = lax.broadcasted_iota(jnp.int32, (left_dim, left_dim), 1)
    goal = ((row >> 1) & 1) * (nz * BW) + (row >> 6) * BW + ((row >> 2) & 15) * 2 + (row & 1)
    perm = jnp.where(goal == col, 1.0, 0.0).astype(BF16)
    lsend[...] = jnp.dot(lf[...].astype(BF16), perm, preferred_element_type=F32).astype(BF16)
    for pj, dev in peers:
        rcopy(lsend, lrecv.at[j], l_ss.at[pj], l_rs.at[j], dev).start()
    lrecv[pl.ds(j, 1)] = lsend[...][None]

    term = lax.broadcasted_iota(jnp.int32, (terms, terms * BW), 0)
    lane = lax.broadcasted_iota(jnp.int32, (terms, terms * BW), 1)
    spread = jnp.where((lane >> 5) == term, 1.0, 0.0).astype(BF16)
    for q in range(PAIR):
        wv[q * 16 : q * 16 + PAIR] = jnp.dot(op_ref[q], spread, preferred_element_type=F32)
    vb[...] = jnp.zeros_like(vb)

    for pj, dev in peers:
        rcopy(psend.at[pj], precv.at[pj], p_ss.at[pj], p_rs.at[pj], dev).wait()
    square = precv[0, 0:1]
    for s in range(1, NS):
        square = square + precv[s, 0:1]
    square = jnp.where(lax.broadcasted_iota(jnp.int32, (1, 128), 1) >= 96, square, 0.0)
    square = square + pltpu.roll(square, 64, 1)
    square = square + pltpu.roll(square, 32, 1)
    for s in range(NS):
        for k in range(4):
            mt[k * 32 + 2 * s : k * 32 + 2 * s + 2] = precv[s, 2 * k : 2 * k + 2]
    flat = mt[...].T
    gbuf[0, pl.ds(i, 1)] = block((flat[0:32], flat[32:64]), pack_last(flat[64:96]))[None]
    start_gather(0)
    zero = jnp.zeros((1, 128), F32)
    start_line(0, [zero, zero, zero, square, zero])

    load_right.wait()
    for part in range(terms * BW // 128):
        rows = rt[part * 4 : part * 4 + 4].reshape(128, rt.shape[2])
        r2[:, part * 128 : part * 128 + 128] = rows.T

    relay(0, zs)
    for pj, dev in peers:
        rcopy(lsend, lrecv.at[pj], l_ss.at[pj], l_rs.at[pj], dev).wait()
    mine = lrecv[...].reshape(NS * terms * 2, left_dim)
    width = 256
    row = lax.broadcasted_iota(jnp.int32, (NS * terms * 2, width), 0)
    col = lax.broadcasted_iota(jnp.int32, (NS * terms * 2, width), 1)
    shift = terms.bit_length()
    goal = ((row & (2 * terms - 1)) >> 1) * BW + (row >> shift) * 2 + (row & 1)
    for part in range(terms * BW // width):
        perm = jnp.where(goal == col + part * width, 1.0, 0.0).astype(BF16)
        lt[:, part * width : part * width + width] = lax.dot_general(
            mine, perm, (((0,), (0,)), ((), ())), preferred_element_type=F32
        ).astype(BF16)
    finish_gather(0)
    alpha, beta = finish_line(0)
    update(0, zero, zero, beta, 0, ng)
    left_and_mix(0)
    right_and_scatter(1)

    def step(t, beta_prev):
        par = t % 2
        start_gather(par)
        start_plane(par, beta_prev)
        start_out(1 - par, early)
        relay(par, zs[:4])
        start_line(par, finish_plane())
        finish_out(t - 1, early)
        relay(par, zs[4:])
        finish_gather(par)
        alpha, beta = finish_line(par)
        alpha_ref[t - 1] = alpha[0, 0]
        beta_ref[t - 1] = beta[0, 0]
        update(par, alpha, beta_prev, beta, 0, ng)
        left_and_mix(par)
        right_and_scatter(1 - par)
        return beta

    beta_prev = lax.fori_loop(1, NUM_STEPS, step, zero)
    par = NUM_STEPS % 2
    start_plane(par, beta_prev)
    start_out(1 - par, early)
    start_line(par, finish_plane())
    finish_out(NUM_STEPS - 1, early)
    alpha, beta = finish_line(par)
    alpha_ref[NUM_STEPS - 1] = alpha[0, 0]
    beta_ref[NUM_STEPS - 1] = beta[0, 0]
    update(par, alpha, beta_prev, beta, i, 1)
    start_out(par, final)
    finish_out(NUM_STEPS, final)


def vmem(n):
    return [pl.BlockSpec(memory_space=pltpu.VMEM)] * n


def dma(*shape):
    return pltpu.SemaphoreType.DMA(shape)


def solution(mesh):
    nz = mesh.shape[ROW] // (NS * NC)
    ng = nz * NC

    def local_run(wave_rows, left_rows, op_pair, right_env):
        terms, rows, left_dim = left_rows.shape
        right_dim = right_env.shape[1]
        count = left_dim * right_dim * PAIR
        nv = NUM_STEPS + 1
        smem = pl.BlockSpec(memory_space=pltpu.SMEM)
        vecs, alpha, beta = pl.pallas_call(
            functools.partial(main_kernel, nz, float(count)),
            out_shape=(
                jax.ShapeDtypeStruct((nv, PAIR, rows, right_dim), F32),
                jax.ShapeDtypeStruct((NUM_STEPS,), F32),
                jax.ShapeDtypeStruct((NUM_STEPS,), F32),
            ),
            in_specs=vmem(3) + [pl.BlockSpec(memory_space=pl.ANY)],
            out_specs=(vmem(1)[0], smem, smem),
            scratch_shapes=[
                pltpu.VMEM((2, ng, BLK, 128), F32),
                pltpu.VMEM((2, ng, BLK, 128), F32),
                pltpu.VMEM((PAIR * BW, left_dim), BF16),
                pltpu.VMEM((PAIR * BW, terms * BW), F32),
                pltpu.VMEM((terms * BW, 384), BF16),
                pltpu.VMEM((NS, BLK, 128), F32),
                pltpu.VMEM((NS, BLK, 128), F32),
                pltpu.VMEM((NS, 8, 128), F32),
                pltpu.VMEM((8, 128), F32),
                pltpu.VMEM((2, ng, 8, 128), F32),
                pltpu.VMEM((left_dim, terms * BW), BF16),
                pltpu.VMEM((right_dim, terms * BW), BF16),
                pltpu.VMEM((PAIR * 16, terms * BW), F32),
                pltpu.VMEM((terms * rows, left_dim), F32),
                pltpu.VMEM((terms * rows, left_dim), BF16),
                pltpu.VMEM((NS, terms * rows, left_dim), BF16),
                pltpu.VMEM((terms, BW, right_dim), BF16),
                pltpu.VMEM((NS, 8, 128), F32),
                pltpu.VMEM((NS, 8, 128), F32),
                pltpu.VMEM((NS, 8, 128), F32),
                pltpu.VMEM((NS, 8, 128), F32),
                pltpu.VMEM((128, 128), F32),
                dma(nz), dma(nz), dma(2, ng), dma(NS), dma(NS), dma(NS), dma(NS), dma(ng), dma(2, ng),
                dma(NS), dma(NS), dma(NS), dma(NS), dma(NS), dma(NS), pltpu.SemaphoreType.DMA,
            ],
            compiler_params=pltpu.CompilerParams(
                collective_id=0, has_side_effects=True, vmem_limit_bytes=56 * 1024 * 1024
            ),
            name="lanczos",
        )(
            wave_rows.transpose(1, 2, 0, 3).reshape(PAIR, rows, right_dim),
            left_rows,
            op_pair.transpose(1, 2, 0),
            right_env,
        )
        vecs = vecs.reshape(nv, 3, 3, rows, right_dim).transpose(0, 3, 1, 2, 4)
        return vecs, alpha, beta

    return jax.shard_map(
        local_run,
        mesh=mesh,
        in_specs=(P(ROW), P(None, ROW), P(), P()),
        out_specs=(P(None, ROW), P(), P()),
        check_vma=False,
    )
```

time: 260 us -> 195 us (0.75)
  Pallas kernels: 226 us -> 190 us
  local copies, waits for them, and re-layouts: 33 us -> 3.87 us
    pallas_call x2 -> x0, Pallas kernels: 35.3 us -> none  [the longest x1 24 us: local_run(): pl.pallas_call(head_kernel, out_shape=(jax.ShapeDtypeStruct((NS, 8, 128),...]
    reshape x20 -> x0, local copies, waits for them, and re-layouts: 16.4 us -> none  [the longest x1 7.79 us: local_run(): left_rows.reshape(terms, rows, nz, NS, NC, rows).transpose(0, 1, 4, 2, 3, 5)]
    transpose x6 -> x0, local copies, waits for them, and re-layouts: 9.1 us -> none  [the longest x1 8.02 us: local_run(): left_rows.reshape(terms, rows, nz, NS, NC, rows).transpose(0, 1, 4, 2, 3, 5)]
where the time goes in v2:
time: 195 us
  Pallas kernels  190 us (97%)
  local copies, waits for them, and re-layouts  3.87 us (2%)
    pallas_call x1, Pallas kernels, local_run(): pl.pallas_call(functools.partial(main_kernel, nz, float(count)), out_shap...  190 us

profile of v2, /device:TPU:1, one launch (start us, length us, event | category | flops | bytes accessed | tf_op | source)
XLA Modules:
  0.0 194.7 jit_solution(8032657933324085486)
XLA Ops:
  0.6 190.2 %lanczos.1 = (f32[7,9,2,512]{3,2,1,0:T(2,128)}, f32[6]{0:T(128)}, f32[6]{0:T(128)}) custom-call(f32[9,2,512]{2,1,0:T(2,128)} %bitcast.8, bf16[32,2,512]{2,1,0:T(2,128)(2,1)} %left_ref.1, bf16[9,9,32]{2,1,0:T(8,128)(2,1)} %bitcast.9, bf16[32,512,512]{2,1,0:T(8,128)(2,1)} %right_ref.1), custom_call_target="tpu_custom_call" | custom-call | tf_op jit(solution)/shard_map/lanczos/pallas_call | solution.py:426
  190.8 1.7 copy.10
  192.5 1.1 copy.11
  193.6 1.1 copy.12

commit v3 on v2

v3 whole, which is shorter than its diff:
```python
import functools

import jax
import jax.numpy as jnp
from jax import lax
from jax.experimental import pallas as pl
from jax.experimental.pallas import tpu as pltpu
from jax.sharding import PartitionSpec as P

NUM_STEPS = 6
ROW = "rows"
NY, NX, NC = 4, 4, 2
NS = NY * NX
PAIR = 9
BW = 32
BLK = 72
HALVES = (slice(0, 32), slice(32, 72))
LANES = 128
TILE, ROWVEC = (8, LANES), (1, LANES)
PAIRED, QUAD = range(2), range(4)
MESH = pl.DeviceIdType.MESH
F32, BF16 = jnp.float32, jnp.bfloat16
OFFSETS = sorted(
    [(dy, dx) for dy in range(NY) for dx in range(NX) if (dy, dx) != (0, 0)],
    key=lambda o: (-(min(o[0], NY - o[0]) + min(o[1], NX - o[1])), o),
)


def span(k, width):
    return slice(k * width, k * width + width)


GROUPS = [(k, span(k, LANES)) for k in QUAD]
ROW0, ROW1, ROW2, ROW3, ROW4 = [span(k, 1) for k in range(5)]


def place():
    me = lax.axis_index(ROW)
    return me // (NS * NC), (me // (NX * NC)) % NY, (me // NC) % NX, me % NC


def device(z, y, x, core):
    return ((z * NY + y) * NX + x) * NC + core


def rcopy(src, dst, send_sem, recv_sem, dev):
    return pltpu.make_async_remote_copy(
        src_ref=src, dst_ref=dst, send_sem=send_sem, recv_sem=recv_sem, device_id=(dev,), device_id_type=MESH
    )


def knock(devs):
    for dev in devs:
        pl.semaphore_signal(pltpu.get_barrier_semaphore(), inc=1, device_id=(dev,), device_id_type=MESH)


def enter(devs):
    pl.semaphore_wait(pltpu.get_barrier_semaphore(), len(devs))


def plane_peers(z, y, x, core):
    out = []
    for dy, dx in OFFSETS:
        py, px = (y + dy) % NY, (x + dx) % NX
        out.append((py * NX + px, device(z, py, px, core)))
    return out


def swap4(a, b, c, d):
    lane = lax.broadcasted_iota(jnp.int32, a.shape, 1)
    low = lane < 64
    even = (lane // 32) % 2 == 0
    a, c = jnp.where(low, a, pltpu.roll(c, 64, 1)), jnp.where(low, pltpu.roll(a, 64, 1), c)
    b, d = jnp.where(low, b, pltpu.roll(d, 64, 1)), jnp.where(low, pltpu.roll(b, 64, 1), d)
    a, b = jnp.where(even, a, pltpu.roll(b, 32, 1)), jnp.where(even, pltpu.roll(a, 96, 1), b)
    c, d = jnp.where(even, c, pltpu.roll(d, 32, 1)), jnp.where(even, pltpu.roll(c, 96, 1), d)
    return a, b, c, d


def fold(val):
    return jnp.sum(val.reshape(BLK // 8, *TILE), axis=0)


def total(val):
    one = jnp.sum(jnp.sum(val, axis=0, keepdims=True), axis=1, keepdims=True)
    return jnp.broadcast_to(one, ROWVEC)


def block(main, last):
    return jnp.concatenate([main[0], main[1], last], axis=0)


def pack_last(rows):
    grp = lax.broadcasted_iota(jnp.int32, TILE, 1) // 32
    packed = rows[0:8]
    for t in range(1, 4):
        packed = jnp.where(grp == t, pltpu.roll(rows[span(t, 8)], 32 * t, 1), packed)
    return packed


def unpack_last(tile):
    return jnp.concatenate([tile if t == 0 else pltpu.roll(tile, 128 - 32 * t, 1) for t in QUAD], axis=0)


def rows5(vals):
    row = lax.broadcasted_iota(jnp.int32, TILE, 0)
    tile = vals[4]
    for k in (3, 2, 1, 0):
        tile = jnp.where(row == k, vals[k], tile)
    return jnp.broadcast_to(tile, TILE)


def ratio(num, den):
    some = den > 0.0
    return jnp.where(some, num / jnp.where(some, den, 1.0), 0.0)


def main_kernel(
    nz, count, psi_ref, left_ref, op_ref, right_ref, vec_ref, ab_ref,
    gbuf, vb, ut, xt, y2, sbuf, rbuf, abuf, asend, cbuf, lt, r2, wv, lf, lsend, lrecv, rt, psend, precv, osend, orecv, mt,
    g_ss, d_ss, g_rs, r_ss, r_rs, a_ss, a_rs, c_ss, c_rs, l_ss, l_rs, p_ss, p_rs, o_ss, o_rs, rt_sem,
):
    ng = nz * NC
    terms = left_ref.shape[0]
    left_dim = left_ref.shape[2]
    z, y, x, core = place()
    i, j = core * nz + z, y * NX + x
    peers = plane_peers(z, y, x, core)
    mate = device(z, y, x, 1 - core)
    zs = [((z + dz) % nz, dz) for dz in sorted(range(1, nz), key=lambda dz: (min(dz, nz - dz), dz))]
    line = [(core, pz, dz) for pz, dz in zs] + [(1 - core, pz, nz + dz) for pz, dz in zs] + [(1 - core, z, nz)]

    load_right = pltpu.make_async_copy(right_ref.at[:, pl.ds(pl.multiple_of(j * BW, BW), BW), :], rt, rt_sem)
    load_right.start()
    others = [dev for _, dev in peers] + [device(pz, y, x, pc) for pc, pz, _ in line]
    knock(others)

    def start_gather(par, half):
        own = gbuf.at[par, i, HALVES[half]]
        for pz, dz in reversed(zs):
            rcopy(own, own, g_ss.at[half, dz], g_rs.at[2 * par + half, i], device(pz, y, x, core)).start()
        rcopy(own, own, g_ss.at[half, 0], g_rs.at[2 * par + half, i], mate).start()

    def relay(par, half):
        for pz, dz in zs:
            slot = core * nz + pz
            ref = gbuf.at[par, slot, HALVES[half]]
            rcopy(ref, ref, g_ss.at[half, dz], g_rs.at[2 * par + half, slot], mate).wait_recv()
            rcopy(ref, ref, d_ss.at[half, dz], g_rs.at[2 * par + half, slot], mate).start()

    def finish_gather(par):
        for half in PAIRED:
            for dz in range(nz):
                slot = (1 - core) * nz + (z + dz) % nz
                ref = gbuf.at[par, slot, HALVES[half]]
                rcopy(ref, ref, g_ss.at[half, 0], g_rs.at[2 * par + half, slot], mate).wait_recv()
        for half in PAIRED:
            own = gbuf.at[par, i, HALVES[half]]
            rcopy(own, own, g_ss.at[half, 0], g_rs.at[2 * par + half, i], mate).wait_send()
            for pz, dz in zs:
                ref = gbuf.at[par, core * nz + pz, HALVES[half]]
                rcopy(own, own, g_ss.at[half, dz], g_rs.at[2 * par + half, i], mate).wait_send()
                rcopy(ref, ref, d_ss.at[half, dz], g_rs.at[2 * par + half, i], mate).wait_send()

    def start_line(par, vals):
        cbuf[par, pl.ds(i, 1)] = rows5(vals)[None]
        own = cbuf.at[par, i]
        for pc, pz, k in line:
            rcopy(own, own, c_ss.at[k], c_rs.at[par, i], device(pz, y, x, pc)).start()

    def finish_line(par):
        own = cbuf.at[par, i]
        for pc, pz, k in line:
            slot = pc * nz + pz
            rcopy(own, cbuf.at[par, slot], c_ss.at[k], c_rs.at[par, slot], mate).wait()
        alpha = cbuf[par, 0, ROW0]
        for s in range(1, ng):
            alpha = alpha + cbuf[par, s, ROW0]
        alpha = alpha / count
        square = jnp.zeros(ROWVEC, F32)
        for s in range(ng):
            off = cbuf[par, s, ROW1] - alpha
            square = square + (cbuf[par, s, ROW3] + 2.0 * (off * cbuf[par, s, ROW4]) + (off * cbuf[par, s, ROW2]) * off)
        return alpha, jnp.sqrt(square / count)

    def start_plane(par, beta_prev):
        w, v, vp = gbuf[par, i], vb[1 - par, i], vb[par, i]
        rest = w - beta_prev * vp
        m, yv, nn = total(fold(w * v)), total(fold(rest * v)), total(fold(v * v))
        p = ratio(yv, nn)
        e = rest - p * v
        tile = rows5([m, p, nn, total(fold(e * e)), total(fold(e * v))])
        asend[...] = tile
        for pj, dev in peers:
            rcopy(asend, abuf.at[j], a_ss.at[pj], a_rs.at[j], dev).start()
        abuf[pl.ds(j, 1)] = tile[None]

    def finish_plane():
        for pj, dev in peers:
            rcopy(asend, abuf.at[pj], a_ss.at[pj], a_rs.at[pj], dev).wait()
        zero = jnp.zeros(ROWVEC, F32)
        m, nn, pn, ee, ev = zero, zero, zero, zero, zero
        for s in range(NS):
            m, nn, pn = m + abuf[s, ROW0], nn + abuf[s, ROW2], pn + abuf[s, ROW1] * abuf[s, ROW2]
        p = ratio(pn, nn)
        for s in range(NS):
            off = abuf[s, ROW1] - p
            ee = ee + (abuf[s, ROW3] + 2.0 * (off * abuf[s, ROW4]) + (off * abuf[s, ROW2]) * off)
            ev = ev + (abuf[s, ROW4] + off * abuf[s, ROW2])
        return [m, p, nn, ee, ev]

    def start_out(par):
        blk = gbuf[par, i]
        last = unpack_last(blk[64:72])
        mt[...] = jnp.concatenate([blk[:64], last, jnp.zeros((32, 128), F32)], axis=0).T
        for pj in range(NS):
            for k in QUAD:
                osend[pj, span(k, 2)] = mt[span(k * NS + pj, 2)]
        for pj, dev in peers:
            rcopy(osend.at[pj], orecv.at[j], o_ss.at[pj], o_rs.at[j], dev).start()
        orecv[pl.ds(j, 1)] = osend[pl.ds(j, 1)]

    def finish_out(num):
        for pj, dev in peers:
            rcopy(osend.at[pj], orecv.at[pj], o_ss.at[pj], o_rs.at[pj], dev).wait()
        for grp, lanes in GROUPS:
            outs = swap4(*[orecv[grp * 4 + k] for k in QUAD])
            for t in PAIRED:
                for k in QUAD:
                    vec_ref[num, 4 * t + k, :, lanes] = outs[t][span(k, 2)]
            vec_ref[num, 8, :, lanes] = outs[2][0:2]

    def own_rows(num, alpha, beta_prev, beta):
        older = num - 2 if isinstance(num, int) else jnp.maximum(num - 2, 0)
        for grp, lanes in GROUPS:
            for q in range(PAIR):
                w, v, vp = vec_ref[num, q, :, lanes], vec_ref[num - 1, q, :, lanes], vec_ref[older, q, :, lanes]
                vec_ref[num, q, :, lanes] = (w - alpha * v - beta_prev * vp) / beta

    def update(par, alpha, beta_prev, beta, first, size):
        def body(s, carry):
            w, v, vp = gbuf[par, s], vb[1 - par, s], vb[par, s]
            vb[par, pl.ds(s, 1)] = ((w - alpha * v - beta_prev * vp) / beta)[None]
            return carry

        lax.fori_loop(first, first + size, body, 0)

    def left(par):
        for grp in range(ng // 4):
            lanes = span(grp, LANES)
            for t in PAIRED:
                outs = swap4(*[vb[par, grp * 4 + ii, span(t, BW)] for ii in QUAD])
                for k in QUAD:
                    q = 4 * t + k
                    ut[span(q, BW), lanes] = outs[k].astype(BF16)
            outs = swap4(*[vb[par, grp * 4 + ii, 64:72] for ii in QUAD])
            ut[256:272, lanes] = jnp.concatenate(outs[:2], axis=0).astype(BF16)
            ut[272:288, lanes] = jnp.concatenate(outs[2:], axis=0).astype(BF16)
        width = 256
        for part in range(terms * BW // width):
            cols = span(part, width)
            whole = jnp.dot(ut[...], lt[:, cols], preferred_element_type=F32)
            xt[:, cols] = whole.astype(BF16).astype(F32)

    def mix(half):
        def body(grp, carry):
            lanes = pl.ds(pl.multiple_of(grp * 128, 128), 128)
            xs = [xt[span(r, BW), lanes] for r in range(PAIR)]

            def one(q):
                acc = wv[q * 16 : q * 16 + 1, lanes] * xs[0]
                for r in range(1, PAIR):
                    acc = acc + wv[q * 16 + r : q * 16 + r + 1, lanes] * xs[r]
                return acc

            rows = [pl.ds(pl.multiple_of(grp * 128 + k * 32, 32), 32) for k in QUAD]
            outs = swap4(*[one(4 * half + k) for k in QUAD])
            for k in QUAD:
                y2[rows[k], span(half, LANES)] = outs[k].astype(BF16)
            if half:
                last = one(8)
                for k in QUAD:
                    moved = last if k == 0 else pltpu.roll(last, 128 - 32 * k, 1)
                    y2[rows[k], 256:384] = moved.astype(BF16)
            return carry

        lax.fori_loop(0, terms * BW // 128, body, 0)

    def start_scatter(half):
        cols = slice(0, 128) if half == 0 else slice(128, 384)
        for dy in (2, 1, 3, 0):
            py = (y + dy) % NY
            part = jnp.dot(
                r2[pl.ds(pl.multiple_of(py * 128, 128), 128), :], y2[:, cols], preferred_element_type=F32
            )
            for px in range(NX):
                pj = py * NX + px
                rows = part[span(px, BW)]
                if half == 0:
                    sbuf[pj, 0:32] = rows
                else:
                    sbuf[pj, 32:64] = rows[:, 0:128]
                    sbuf[pj, 64:72] = pack_last(rows[:, 128:256])
                send = rcopy(
                    sbuf.at[pj, HALVES[half]], rbuf.at[j, HALVES[half]],
                    r_ss.at[half, pj], r_rs.at[half, j], device(z, py, px, core),
                )
                if dy:
                    send.start()
                else:

                    @pl.when(px != x)
                    def _():
                        send.start()

        rbuf[pl.ds(j, 1), HALVES[half]] = sbuf[pl.ds(j, 1), HALVES[half]]

    def finish_scatter(nxt, half):
        for pj, dev in reversed(peers):
            rcopy(
                sbuf.at[pj, HALVES[half]], rbuf.at[pj, HALVES[half]], r_ss.at[half, pj], r_rs.at[half, pj], dev
            ).wait()
        w = rbuf[0, HALVES[half]]
        for s in range(1, NS):
            w = w + rbuf[s, HALVES[half]]
        gbuf[nxt, pl.ds(i, 1), HALVES[half]] = w[None]

    def product(par, nxt, more, between):
        left(par)
        for half in PAIRED:
            mix(half)
            start_scatter(half)
        between()
        for half in PAIRED:
            finish_scatter(nxt, half)
            if more is True:
                start_gather(nxt, half)
            else:

                @pl.when(more)
                def _(half=half):
                    start_gather(nxt, half)

    norm = jnp.zeros(ROWVEC, F32)
    for grp, lanes in GROUPS:
        for q in range(PAIR):
            norm = norm + jnp.sum(psi_ref[q, :, lanes] * psi_ref[q, :, lanes], axis=0, keepdims=True)
    norm = jnp.broadcast_to(jnp.sum(norm, axis=1, keepdims=True), TILE)
    for t in range(3):
        mt[span(t, 8)] = jnp.zeros(TILE, F32)
    for grp, lanes in GROUPS:
        for q in range(PAIR):
            mt[span(q, 2)] = psi_ref[q, :, lanes]
        outs = swap4(mt[0:8], mt[8:16], mt[16:24], norm)
        for k in QUAD:
            psend[grp * 4 + k] = outs[k]
    enter(others)
    for pj, dev in peers:
        rcopy(psend.at[pj], precv.at[j], p_ss.at[pj], p_rs.at[j], dev).start()
    precv[pl.ds(j, 1)] = psend[pl.ds(j, 1)]

    for k in range(terms):
        lf[span(k, 2)] = left_ref[k].astype(F32)
    row = lax.broadcasted_iota(jnp.int32, (left_dim, left_dim), 0)
    col = lax.broadcasted_iota(jnp.int32, (left_dim, left_dim), 1)
    goal = ((row >> 1) & 1) * (nz * BW) + (row >> 6) * BW + ((row >> 2) & 15) * 2 + (row & 1)
    perm = jnp.where(goal == col, 1.0, 0.0).astype(BF16)
    lsend[...] = jnp.dot(lf[...].astype(BF16), perm, preferred_element_type=F32).astype(BF16)
    for pj, dev in peers:
        rcopy(lsend, lrecv.at[j], l_ss.at[pj], l_rs.at[j], dev).start()
    lrecv[pl.ds(j, 1)] = lsend[...][None]

    term = lax.broadcasted_iota(jnp.int32, (terms, terms * BW), 0)
    lane = lax.broadcasted_iota(jnp.int32, (terms, terms * BW), 1)
    spread = jnp.where((lane >> 5) == term, 1.0, 0.0).astype(BF16)
    for q in range(PAIR):
        wv[q * 16 : q * 16 + PAIR] = jnp.dot(op_ref[q], spread, preferred_element_type=F32)
    vb[...] = jnp.zeros_like(vb)

    for pj, dev in peers:
        rcopy(psend.at[pj], precv.at[pj], p_ss.at[pj], p_rs.at[pj], dev).wait()
    square = precv[0, ROW0]
    for s in range(1, NS):
        square = square + precv[s, ROW0]
    square = jnp.where(lax.broadcasted_iota(jnp.int32, ROWVEC, 1) >= 96, square, 0.0)
    square = square + pltpu.roll(square, 64, 1)
    square = square + pltpu.roll(square, 32, 1)
    for s in range(NS):
        for k in QUAD:
            mt[span(k * NS + s, 2)] = precv[s, span(k, 2)]
    flat = mt[...].T
    gbuf[0, pl.ds(i, 1)] = block((flat[span(0, BW)], flat[span(1, BW)]), pack_last(flat[span(2, BW)]))[None]
    start_gather(0, 0)
    start_gather(0, 1)
    zero = jnp.zeros(ROWVEC, F32)
    start_line(0, [zero, zero, zero, square, zero])

    load_right.wait()
    for part in range(terms * BW // 128):
        rows = rt[span(part, 4)].reshape(128, rt.shape[2])
        r2[:, span(part, LANES)] = rows.T

    relay(0, 0)
    relay(0, 1)
    for pj, dev in peers:
        rcopy(lsend, lrecv.at[pj], l_ss.at[pj], l_rs.at[pj], dev).wait()
    mine = lrecv[...].reshape(NS * terms * 2, left_dim)
    width = 256
    row = lax.broadcasted_iota(jnp.int32, (NS * terms * 2, width), 0)
    col = lax.broadcasted_iota(jnp.int32, (NS * terms * 2, width), 1)
    shift = terms.bit_length()
    goal = ((row & (2 * terms - 1)) >> 1) * BW + (row >> shift) * 2 + (row & 1)
    for part in range(terms * BW // width):
        perm = jnp.where(goal == col + part * width, 1.0, 0.0).astype(BF16)
        lt[:, span(part, width)] = lax.dot_general(
            mine, perm, (((0,), (0,)), ((), ())), preferred_element_type=F32
        ).astype(BF16)
    finish_gather(0)
    alpha, beta = finish_line(0)
    update(0, zero, zero, beta, 0, ng)

    def first_rows():
        for grp, lanes in GROUPS:
            for q in range(PAIR):
                vec_ref[0, q, :, lanes] = psi_ref[q, :, lanes] / beta

    product(0, 1, True, first_rows)

    def step(t, beta_prev):
        par = t % 2
        start_plane(par, beta_prev)
        start_out(par)
        relay(par, 0)
        start_line(par, finish_plane())
        relay(par, 1)
        finish_out(t)
        finish_gather(par)
        alpha, beta = finish_line(par)
        update(par, alpha, beta_prev, beta, 0, ng)

        def rest():
            ab_ref[0, t - 1] = alpha[0, 0]
            ab_ref[1, t - 1] = beta[0, 0]
            own_rows(t, alpha, beta_prev, beta)

        product(par, 1 - par, t < NUM_STEPS - 1, rest)
        return beta

    beta_prev = lax.fori_loop(1, NUM_STEPS, step, zero)
    par = NUM_STEPS % 2
    start_plane(par, beta_prev)
    start_out(par)
    start_line(par, finish_plane())
    finish_out(NUM_STEPS)
    alpha, beta = finish_line(par)
    ab_ref[0, NUM_STEPS - 1] = alpha[0, 0]
    ab_ref[1, NUM_STEPS - 1] = beta[0, 0]
    own_rows(NUM_STEPS, alpha, beta_prev, beta)


def vmem(n):
    return [pl.BlockSpec(memory_space=pltpu.VMEM)] * n


def dma(*shape):
    return pltpu.SemaphoreType.DMA(shape)


def solution(mesh):
    nz = mesh.shape[ROW] // (NS * NC)
    ng = nz * NC

    def local_run(wave_rows, left_rows, op_pair, right_env):
        terms, rows, left_dim = left_rows.shape
        right_dim = right_env.shape[1]
        count = left_dim * right_dim * PAIR
        nv = NUM_STEPS + 1
        smem = pl.BlockSpec(memory_space=pltpu.SMEM)
        vecs, ab = pl.pallas_call(
            functools.partial(main_kernel, nz, float(count)),
            out_shape=(
                jax.ShapeDtypeStruct((nv, PAIR, rows, right_dim), F32),
                jax.ShapeDtypeStruct((2, NUM_STEPS), F32),
            ),
            in_specs=vmem(3) + [pl.BlockSpec(memory_space=pl.ANY)],
            out_specs=(vmem(1)[0], smem),
            scratch_shapes=[
                pltpu.VMEM((2, ng, BLK, LANES), F32),
                pltpu.VMEM((2, ng, BLK, LANES), F32),
                pltpu.VMEM((PAIR * BW, left_dim), BF16),
                pltpu.VMEM((PAIR * BW, terms * BW), F32),
                pltpu.VMEM((terms * BW, 384), BF16),
                pltpu.VMEM((NS, BLK, LANES), F32),
                pltpu.VMEM((NS, BLK, LANES), F32),
                pltpu.VMEM((NS, *TILE), F32),
                pltpu.VMEM(TILE, F32),
                pltpu.VMEM((2, ng, *TILE), F32),
                pltpu.VMEM((left_dim, terms * BW), BF16),
                pltpu.VMEM((right_dim, terms * BW), BF16),
                pltpu.VMEM((PAIR * 16, terms * BW), F32),
                pltpu.VMEM((terms * rows, left_dim), F32),
                pltpu.VMEM((terms * rows, left_dim), BF16),
                pltpu.VMEM((NS, terms * rows, left_dim), BF16),
                pltpu.VMEM((terms, BW, right_dim), BF16),
                pltpu.VMEM((NS, *TILE), F32),
                pltpu.VMEM((NS, *TILE), F32),
                pltpu.VMEM((NS, *TILE), F32),
                pltpu.VMEM((NS, *TILE), F32),
                pltpu.VMEM((128, 128), F32),
                dma(2, nz), dma(2, nz), dma(4, ng), dma(2, NS), dma(2, NS), dma(NS), dma(NS), dma(ng), dma(2, ng),
                dma(NS), dma(NS), dma(NS), dma(NS), dma(NS), dma(NS), pltpu.SemaphoreType.DMA,
            ],
            compiler_params=pltpu.CompilerParams(
                collective_id=0, has_side_effects=True, vmem_limit_bytes=56 * 1024 * 1024
            ),
            name="lanczos",
        )(
            wave_rows.transpose(1, 2, 0, 3).reshape(PAIR, rows, right_dim),
            left_rows,
            op_pair.transpose(1, 2, 0),
            right_env,
        )
        vecs = vecs.reshape(nv, 3, 3, rows, right_dim).transpose(0, 3, 1, 2, 4)
        return vecs, ab[0], ab[1]

    return jax.shard_map(
        local_run,
        mesh=mesh,
        in_specs=(P(ROW), P(None, ROW), P(), P()),
        out_specs=(P(None, ROW), P(), P()),
        check_vma=False,
    )
```

time: 195 us -> 172 us (0.88)
  Pallas kernels: 190 us -> 168 us
    pallas_call x1, Pallas kernels: 190 us -> 168 us  [local_run(): pl.pallas_call(functools.partial(main_kernel, nz, float(count)), out_shap...]
    unnamed x3 -> x1, local copies, waits for them, and re-layouts: 3.87 us -> 1.66 us
where the time goes in v3:
time: 172 us
  Pallas kernels  168 us (98%)
  local copies, waits for them, and re-layouts  2.92 us (2%)
    pallas_call x1, Pallas kernels, local_run(): pl.pallas_call(functools.partial(main_kernel, nz, float(count)), out_shap...  168 us

profile of v3, /device:TPU:1, one launch (start us, length us, event | category | flops | bytes accessed | tf_op | source)
XLA Modules:
  0.0 171.9 jit_solution(11348984324040866339)
XLA Ops:
  0.6 168.3 %lanczos.1 = (f32[7,9,2,512]{3,2,1,0:T(2,128)}, f32[2,6]{1,0:T(2,128)}) custom-call(f32[9,2,512]{2,1,0:T(2,128)} %bitcast.12, bf16[32,2,512]{2,1,0:T(2,128)(2,1)} %left_ref.1, bf16[9,9,32]{2,1,0:T(8,128)(2,1)} %bitcast.13, bf16[32,512,512]{2,1,0:T(8,128)(2,1)} %right_ref.1), custom_call_target="tpu_custom_call" | custom-call | tf_op jit(solution)/shard_map/lanczos/pallas_call | solution.py:479
  168.9 1.3 slice_bitcast_fusion
  170.2 1.7 copy.8

commit v4 on v3

--- a/solution.py
+++ b/solution.py
@@ -154,6 +154,7 @@
                 slot = (1 - core) * nz + (z + dz) % nz
                 ref = gbuf.at[par, slot, HALVES[half]]
                 rcopy(ref, ref, g_ss.at[half, 0], g_rs.at[2 * par + half, slot], mate).wait_recv()
+    def drain_gather(par):
         for half in PAIRED:
             own = gbuf.at[par, i, HALVES[half]]
             rcopy(own, own, g_ss.at[half, 0], g_rs.at[2 * par + half, i], mate).wait_send()
@@ -243,9 +244,9 @@
             vb[par, pl.ds(s, 1)] = ((w - alpha * v - beta_prev * vp) / beta)[None]
             return carry
 
-        lax.fori_loop(first, first + size, body, 0)
-
-    def left(par):
+        lax.fori_loop(first, first + size, body, 0, unroll=4 if size > 1 else 1)
+
+    def left_and_mix(par):
         for grp in range(ng // 4):
             lanes = span(grp, LANES)
             for t in PAIRED:
@@ -259,32 +260,37 @@
         width = 256
         for part in range(terms * BW // width):
             cols = span(part, width)
-            whole = jnp.dot(ut[...], lt[:, cols], preferred_element_type=F32)
-            xt[:, cols] = whole.astype(BF16).astype(F32)
-
-    def mix(half):
+            whole = jnp.dot(ut[...], lt[:, cols], preferred_element_type=F32).astype(BF16).astype(F32)
+            xt[:, cols] = whole
+            for sub in range(width // LANES):
+                grp = part * (width // LANES) + sub
+                mix(0, [whole[span(r, BW), span(sub, LANES)] for r in range(PAIR)], span(grp, LANES), grp * LANES)
+
+    def mix(half, xs, lanes, first):
+        def one(q):
+            acc = wv[q * 16 : q * 16 + 1, lanes] * xs[0]
+            for r in range(1, PAIR):
+                acc = acc + wv[q * 16 + r : q * 16 + r + 1, lanes] * xs[r]
+            return acc
+
+        rows = [pl.ds(first + k * BW, BW) for k in QUAD]
+        outs = swap4(*[one(4 * half + k) for k in QUAD])
+        for k in QUAD:
+            y2[rows[k], span(half, LANES)] = outs[k].astype(BF16)
+        if half:
+            last = one(8)
+            for k in QUAD:
+                moved = last if k == 0 else pltpu.roll(last, LANES - BW * k, 1)
+                y2[rows[k], 2 * LANES :] = moved.astype(BF16)
+
+    def mix_rest():
         def body(grp, carry):
-            lanes = pl.ds(pl.multiple_of(grp * 128, 128), 128)
-            xs = [xt[span(r, BW), lanes] for r in range(PAIR)]
-
-            def one(q):
-                acc = wv[q * 16 : q * 16 + 1, lanes] * xs[0]
-                for r in range(1, PAIR):
-                    acc = acc + wv[q * 16 + r : q * 16 + r + 1, lanes] * xs[r]
-                return acc
-
-            rows = [pl.ds(pl.multiple_of(grp * 128 + k * 32, 32), 32) for k in QUAD]
-            outs = swap4(*[one(4 * half + k) for k in QUAD])
-            for k in QUAD:
-                y2[rows[k], span(half, LANES)] = outs[k].astype(BF16)
-            if half:
-                last = one(8)
-                for k in QUAD:
-                    moved = last if k == 0 else pltpu.roll(last, 128 - 32 * k, 1)
-                    y2[rows[k], 256:384] = moved.astype(BF16)
+            first = pl.multiple_of(grp * LANES, LANES)
+            lanes = pl.ds(first, LANES)
+            mix(1, [xt[span(r, BW), lanes] for r in range(PAIR)], lanes, first)
             return carry
 
-        lax.fori_loop(0, terms * BW // 128, body, 0)
+        lax.fori_loop(0, terms * BW // LANES, body, 0, unroll=2)
 
     def start_scatter(half):
         cols = slice(0, 128) if half == 0 else slice(128, 384)
@@ -326,10 +332,11 @@
         gbuf[nxt, pl.ds(i, 1), HALVES[half]] = w[None]
 
     def product(par, nxt, more, between):
-        left(par)
-        for half in PAIRED:
-            mix(half)
-            start_scatter(half)
+        left_and_mix(par)
+        start_scatter(0)
+        mix_rest()
+        start_scatter(1)
+        drain_gather(par)
         between()
         for half in PAIRED:
             finish_scatter(nxt, half)

time: 172 us -> 162 us (0.942)
  Pallas kernels: 168 us -> 158 us
    pallas_call x1, Pallas kernels: 168 us -> 158 us  [local_run(): pl.pallas_call(functools.partial(main_kernel, nz, float(count)), out_shap...]
where the time goes in v4:
time: 162 us
  Pallas kernels  158 us (98%)
  local copies, waits for them, and re-layouts  2.92 us (2%)
    pallas_call x1, Pallas kernels, local_run(): pl.pallas_call(functools.partial(main_kernel, nz, float(count)), out_shap...  158 us

profile of v4, /device:TPU:1, one launch (start us, length us, event | category | flops | bytes accessed | tf_op | source)
XLA Modules:
  0.0 161.5 jit_solution(4521353753334455255)
XLA Ops:
  0.6 158.0 %lanczos.1 = (f32[7,9,2,512]{3,2,1,0:T(2,128)}, f32[2,6]{1,0:T(2,128)}) custom-call(f32[9,2,512]{2,1,0:T(2,128)} %bitcast.12, bf16[32,2,512]{2,1,0:T(2,128)(2,1)} %left_ref.1, bf16[9,9,32]{2,1,0:T(8,128)(2,1)} %bitcast.13, bf16[32,512,512]{2,1,0:T(8,128)(2,1)} %right_ref.1), custom_call_target="tpu_custom_call" | custom-call | tf_op jit(solution)/shard_map/lanczos/pallas_call | solution.py:486
  158.6 1.3 slice_bitcast_fusion
  159.9 1.7 %copy.8 = f32[7,2,3,3,512]{4,1,3,2,0:T(2,128)} copy(f32[7,2,3,3,512]{4,1,3,2,0:T(2,128)} %bitcast.11) | data formatting | bytes 516096

commit v5 on v4

--- a/solution.py
+++ b/solution.py
@@ -164,7 +164,11 @@
                 rcopy(ref, ref, d_ss.at[half, dz], g_rs.at[2 * par + half, i], mate).wait_send()
 
     def start_line(par, vals):
-        cbuf[par, pl.ds(i, 1)] = rows5(vals)[None]
+        lane = lax.broadcasted_iota(jnp.int32, ROWVEC, 1)
+        line_row = vals[4]
+        for k in reversed(QUAD):
+            line_row = jnp.where(lane == k, vals[k], line_row)
+        cbuf[par, pl.ds(i, 1)] = line_row[None]
         own = cbuf.at[par, i]
         for pc, pz, k in line:
             rcopy(own, own, c_ss.at[k], c_rs.at[par, i], device(pz, y, x, pc)).start()
@@ -174,15 +178,13 @@
         for pc, pz, k in line:
             slot = pc * nz + pz
             rcopy(own, cbuf.at[par, slot], c_ss.at[k], c_rs.at[par, slot], mate).wait()
-        alpha = cbuf[par, 0, ROW0]
-        for s in range(1, ng):
-            alpha = alpha + cbuf[par, s, ROW0]
-        alpha = alpha / count
-        square = jnp.zeros(ROWVEC, F32)
-        for s in range(ng):
-            off = cbuf[par, s, ROW1] - alpha
-            square = square + (cbuf[par, s, ROW3] + 2.0 * (off * cbuf[par, s, ROW4]) + (off * cbuf[par, s, ROW2]) * off)
-        return alpha, jnp.sqrt(square / count)
+        rows = jnp.concatenate([cbuf[par, s] for s in range(ng)], axis=0)
+        lane = lax.broadcasted_iota(jnp.int32, rows.shape, 1)
+        m, p, nn, ee, ev = [jnp.sum(jnp.where(lane == k, rows, 0.0), axis=1, keepdims=True) for k in range(5)]
+        alpha = jnp.sum(m, axis=0, keepdims=True) / count
+        off = p - alpha
+        square = jnp.sum(ee + 2.0 * (off * ev) + (off * nn) * off, axis=0, keepdims=True)
+        return jnp.broadcast_to(alpha, ROWVEC), jnp.broadcast_to(jnp.sqrt(square / count), ROWVEC)
 
     def start_plane(par, beta_prev):
         w, v, vp = gbuf[par, i], vb[1 - par, i], vb[par, i]
@@ -408,7 +410,6 @@
         r2[:, span(part, LANES)] = rows.T
 
     relay(0, 0)
-    relay(0, 1)
     for pj, dev in peers:
         rcopy(lsend, lrecv.at[pj], l_ss.at[pj], l_rs.at[pj], dev).wait()
     mine = lrecv[...].reshape(NS * terms * 2, left_dim)
@@ -422,6 +423,7 @@
         lt[:, span(part, width)] = lax.dot_general(
             mine, perm, (((0,), (0,)), ((), ())), preferred_element_type=F32
         ).astype(BF16)
+    relay(0, 1)
     finish_gather(0)
     alpha, beta = finish_line(0)
     update(0, zero, zero, beta, 0, ng)
@@ -501,7 +503,7 @@
                 pltpu.VMEM((NS, BLK, LANES), F32),
                 pltpu.VMEM((NS, *TILE), F32),
                 pltpu.VMEM(TILE, F32),
-                pltpu.VMEM((2, ng, *TILE), F32),
+                pltpu.VMEM((2, ng, *ROWVEC), F32),
                 pltpu.VMEM((left_dim, terms * BW), BF16),
                 pltpu.VMEM((right_dim, terms * BW), BF16),
                 pltpu.VMEM((PAIR * 16, terms * BW), F32),

time: 162 us -> 164 us (1.012)
  Pallas kernels: 158 us -> 161 us
    pallas_call x1, Pallas kernels: 158 us -> 161 us  [local_run(): pl.pallas_call(functools.partial(main_kernel, nz, float(count)), out_shap...]
where the time goes in v5:
time: 164 us
  Pallas kernels  161 us (98%)
  local copies, waits for them, and re-layouts  2.92 us (2%)
    pallas_call x1, Pallas kernels, local_run(): pl.pallas_call(functools.partial(main_kernel, nz, float(count)), out_shap...  161 us

profile of v5, /device:TPU:1, one launch (start us, length us, event | category | flops | bytes accessed | tf_op | source)
XLA Modules:
  0.0 164.1 jit_solution(6046846237582650477)
XLA Ops:
  0.6 160.5 %lanczos.1 = (f32[7,9,2,512]{3,2,1,0:T(2,128)}, f32[2,6]{1,0:T(2,128)}) custom-call(f32[9,2,512]{2,1,0:T(2,128)} %bitcast.12, bf16[32,2,512]{2,1,0:T(2,128)(2,1)} %left_ref.1, bf16[9,9,32]{2,1,0:T(8,128)(2,1)} %bitcast.13, bf16[32,512,512]{2,1,0:T(8,128)(2,1)} %right_ref.1), custom_call_target="tpu_custom_call" | custom-call | tf_op jit(solution)/shard_map/lanczos/pallas_call | solution.py:488
  161.2 1.3 slice_bitcast_fusion
  162.4 1.7 %copy.8 = f32[7,2,3,3,512]{4,1,3,2,0:T(2,128)} copy(f32[7,2,3,3,512]{4,1,3,2,0:T(2,128)} %bitcast.11) | data formatting | bytes 516096

commit v6 on v5

--- a/solution.py
+++ b/solution.py
@@ -266,33 +266,32 @@
             xt[:, cols] = whole
             for sub in range(width // LANES):
                 grp = part * (width // LANES) + sub
-                mix(0, [whole[span(r, BW), span(sub, LANES)] for r in range(PAIR)], span(grp, LANES), grp * LANES)
-
-    def mix(half, xs, lanes, first):
-        def one(q):
-            acc = wv[q * 16 : q * 16 + 1, lanes] * xs[0]
-            for r in range(1, PAIR):
-                acc = acc + wv[q * 16 + r : q * 16 + r + 1, lanes] * xs[r]
-            return acc
-
-        rows = [pl.ds(first + k * BW, BW) for k in QUAD]
-        outs = swap4(*[one(4 * half + k) for k in QUAD])
-        for k in QUAD:
-            y2[rows[k], span(half, LANES)] = outs[k].astype(BF16)
-        if half:
-            last = one(8)
+                mix(0, grp, [whole[span(r, BW), span(sub, LANES)] for r in range(PAIR)])
+
+    def mix(half, grp, xs):
+        lanes = span(grp, LANES)
+        for part in PAIRED:
+            some = [x_r[span(part, 16)] for x_r in xs]
+
+            def one(q):
+                acc = wv[q * 16 : q * 16 + 1, lanes] * some[0]
+                for r in range(1, PAIR):
+                    acc = acc + wv[q * 16 + r : q * 16 + r + 1, lanes] * some[r]
+                return acc
+
+            rows = [span(grp * 8 + 2 * k + part, 16) for k in QUAD]
+            outs = swap4(*[one(4 * half + k) for k in QUAD])
             for k in QUAD:
-                moved = last if k == 0 else pltpu.roll(last, LANES - BW * k, 1)
-                y2[rows[k], 2 * LANES :] = moved.astype(BF16)
+                y2[rows[k], span(half, LANES)] = outs[k].astype(BF16)
+            if half:
+                last = one(8)
+                for k in QUAD:
+                    moved = last if k == 0 else pltpu.roll(last, LANES - BW * k, 1)
+                    y2[rows[k], 2 * LANES :] = moved.astype(BF16)
 
     def mix_rest():
-        def body(grp, carry):
-            first = pl.multiple_of(grp * LANES, LANES)
-            lanes = pl.ds(first, LANES)
-            mix(1, [xt[span(r, BW), lanes] for r in range(PAIR)], lanes, first)
-            return carry
-
-        lax.fori_loop(0, terms * BW // LANES, body, 0, unroll=2)
+        for grp in range(terms * BW // LANES):
+            mix(1, grp, [xt[span(r, BW), span(grp, LANES)] for r in range(PAIR)])
 
     def start_scatter(half):
         cols = slice(0, 128) if half == 0 else slice(128, 384)
@@ -410,6 +409,7 @@
         r2[:, span(part, LANES)] = rows.T
 
     relay(0, 0)
+    relay(0, 1)
     for pj, dev in peers:
         rcopy(lsend, lrecv.at[pj], l_ss.at[pj], l_rs.at[pj], dev).wait()
     mine = lrecv[...].reshape(NS * terms * 2, left_dim)
@@ -423,7 +423,6 @@
         lt[:, span(part, width)] = lax.dot_general(
             mine, perm, (((0,), (0,)), ((), ())), preferred_element_type=F32
         ).astype(BF16)
-    relay(0, 1)
     finish_gather(0)
     alpha, beta = finish_line(0)
     update(0, zero, zero, beta, 0, ng)

time: 164 us -> 162 us (0.988)
  Pallas kernels: 161 us -> 158 us
    pallas_call x1, Pallas kernels: 161 us -> 158 us  [local_run(): pl.pallas_call(functools.partial(main_kernel, nz, float(count)), out_shap...]
where the time goes in v6:
time: 162 us
  Pallas kernels  158 us (98%)
  local copies, waits for them, and re-layouts  2.92 us (2%)
    pallas_call x1, Pallas kernels, local_run(): pl.pallas_call(functools.partial(main_kernel, nz, float(count)), out_shap...  158 us

profile of v6, /device:TPU:1, one launch (start us, length us, event | category | flops | bytes accessed | tf_op | source)
XLA Modules:
  0.0 161.5 jit_solution(6272796289843560287)
XLA Ops:
  0.6 158.0 %lanczos.1 = (f32[7,9,2,512]{3,2,1,0:T(2,128)}, f32[2,6]{1,0:T(2,128)}) custom-call(f32[9,2,512]{2,1,0:T(2,128)} %bitcast.12, bf16[32,2,512]{2,1,0:T(2,128)(2,1)} %left_ref.1, bf16[9,9,32]{2,1,0:T(8,128)(2,1)} %bitcast.13, bf16[32,512,512]{2,1,0:T(8,128)(2,1)} %right_ref.1), custom_call_target="tpu_custom_call" | custom-call | tf_op jit(solution)/shard_map/lanczos/pallas_call | solution.py:487
  158.6 1.3 slice_bitcast_fusion
  159.9 1.7 %copy.8 = f32[7,2,3,3,512]{4,1,3,2,0:T(2,128)} copy(f32[7,2,3,3,512]{4,1,3,2,0:T(2,128)} %bitcast.11) | data formatting | bytes 516096

commit v7 on v6

--- a/solution.py
+++ b/solution.py
@@ -177,7 +177,7 @@
         own = cbuf.at[par, i]
         for pc, pz, k in line:
             slot = pc * nz + pz
-            rcopy(own, cbuf.at[par, slot], c_ss.at[k], c_rs.at[par, slot], mate).wait()
+            rcopy(own, cbuf.at[par, slot], c_ss.at[k], c_rs.at[par, slot], mate).wait_recv()
         rows = jnp.concatenate([cbuf[par, s] for s in range(ng)], axis=0)
         lane = lax.broadcasted_iota(jnp.int32, rows.shape, 1)
         m, p, nn, ee, ev = [jnp.sum(jnp.where(lane == k, rows, 0.0), axis=1, keepdims=True) for k in range(5)]
@@ -200,7 +200,7 @@
 
     def finish_plane():
         for pj, dev in peers:
-            rcopy(asend, abuf.at[pj], a_ss.at[pj], a_rs.at[pj], dev).wait()
+            rcopy(asend, abuf.at[pj], a_ss.at[pj], a_rs.at[pj], dev).wait_recv()
         zero = jnp.zeros(ROWVEC, F32)
         m, nn, pn, ee, ev = zero, zero, zero, zero, zero
         for s in range(NS):
@@ -225,7 +225,7 @@
 
     def finish_out(num):
         for pj, dev in peers:
-            rcopy(osend.at[pj], orecv.at[pj], o_ss.at[pj], o_rs.at[pj], dev).wait()
+            rcopy(osend.at[pj], orecv.at[pj], o_ss.at[pj], o_rs.at[pj], dev).wait_recv()
         for grp, lanes in GROUPS:
             outs = swap4(*[orecv[grp * 4 + k] for k in QUAD])
             for t in PAIRED:
@@ -326,11 +326,28 @@
         for pj, dev in reversed(peers):
             rcopy(
                 sbuf.at[pj, HALVES[half]], rbuf.at[pj, HALVES[half]], r_ss.at[half, pj], r_rs.at[half, pj], dev
-            ).wait()
+            ).wait_recv()
         w = rbuf[0, HALVES[half]]
         for s in range(1, NS):
             w = w + rbuf[s, HALVES[half]]
         gbuf[nxt, pl.ds(i, 1), HALVES[half]] = w[None]
+
+    def drain_sums(par):
+        for pj, dev in peers:
+            rcopy(asend, abuf.at[pj], a_ss.at[pj], a_rs.at[pj], dev).wait_send()
+            rcopy(osend.at[pj], orecv.at[pj], o_ss.at[pj], o_rs.at[pj], dev).wait_send()
+        drain_line(par)
+
+    def drain_line(par):
+        own = cbuf.at[par, i]
+        for pc, pz, k in line:
+            rcopy(own, own, c_ss.at[k], c_rs.at[par, i], mate).wait_send()
+
+    def drain_scatter():
+        for half in PAIRED:
+            for pj, dev in peers:
+                ref = sbuf.at[pj, HALVES[half]]
+                rcopy(ref, ref, r_ss.at[half, pj], r_rs.at[half, pj], dev).wait_send()
 
     def product(par, nxt, more, between):
         left_and_mix(par)
@@ -362,11 +379,6 @@
         outs = swap4(mt[0:8], mt[8:16], mt[16:24], norm)
         for k in QUAD:
             psend[grp * 4 + k] = outs[k]
-    enter(others)
-    for pj, dev in peers:
-        rcopy(psend.at[pj], precv.at[j], p_ss.at[pj], p_rs.at[j], dev).start()
-    precv[pl.ds(j, 1)] = psend[pl.ds(j, 1)]
-
     for k in range(terms):
         lf[span(k, 2)] = left_ref[k].astype(F32)
     row = lax.broadcasted_iota(jnp.int32, (left_dim, left_dim), 0)
@@ -374,6 +386,10 @@
     goal = ((row >> 1) & 1) * (nz * BW) + (row >> 6) * BW + ((row >> 2) & 15) * 2 + (row & 1)
     perm = jnp.where(goal == col, 1.0, 0.0).astype(BF16)
     lsend[...] = jnp.dot(lf[...].astype(BF16), perm, preferred_element_type=F32).astype(BF16)
+    enter(others)
+    for pj, dev in peers:
+        rcopy(psend.at[pj], precv.at[j], p_ss.at[pj], p_rs.at[j], dev).start()
+    precv[pl.ds(j, 1)] = psend[pl.ds(j, 1)]
     for pj, dev in peers:
         rcopy(lsend, lrecv.at[j], l_ss.at[pj], l_rs.at[j], dev).start()
     lrecv[pl.ds(j, 1)] = lsend[...][None]
@@ -386,7 +402,7 @@
     vb[...] = jnp.zeros_like(vb)
 
     for pj, dev in peers:
-        rcopy(psend.at[pj], precv.at[pj], p_ss.at[pj], p_rs.at[pj], dev).wait()
+        rcopy(psend.at[pj], precv.at[pj], p_ss.at[pj], p_rs.at[pj], dev).wait_recv()
     square = precv[0, ROW0]
     for s in range(1, NS):
         square = square + precv[s, ROW0]
@@ -411,7 +427,7 @@
     relay(0, 0)
     relay(0, 1)
     for pj, dev in peers:
-        rcopy(lsend, lrecv.at[pj], l_ss.at[pj], l_rs.at[pj], dev).wait()
+        rcopy(lsend, lrecv.at[pj], l_ss.at[pj], l_rs.at[pj], dev).wait_recv()
     mine = lrecv[...].reshape(NS * terms * 2, left_dim)
     width = 256
     row = lax.broadcasted_iota(jnp.int32, (NS * terms * 2, width), 0)
@@ -428,6 +444,10 @@
     update(0, zero, zero, beta, 0, ng)
 
     def first_rows():
+        drain_line(0)
+        for pj, dev in peers:
+            rcopy(psend.at[pj], precv.at[pj], p_ss.at[pj], p_rs.at[pj], dev).wait_send()
+            rcopy(lsend, lrecv.at[pj], l_ss.at[pj], l_rs.at[pj], dev).wait_send()
         for grp, lanes in GROUPS:
             for q in range(PAIR):
                 vec_ref[0, q, :, lanes] = psi_ref[q, :, lanes] / beta
@@ -438,6 +458,7 @@
         par = t % 2
         start_plane(par, beta_prev)
         start_out(par)
+        drain_scatter()
         relay(par, 0)
         start_line(par, finish_plane())
         relay(par, 1)
@@ -447,6 +468,7 @@
         update(par, alpha, beta_prev, beta, 0, ng)
 
         def rest():
+            drain_sums(par)
             ab_ref[0, t - 1] = alpha[0, 0]
             ab_ref[1, t - 1] = beta[0, 0]
             own_rows(t, alpha, beta_prev, beta)
@@ -458,12 +480,21 @@
     par = NUM_STEPS % 2
     start_plane(par, beta_prev)
     start_out(par)
+    drain_scatter()
     start_line(par, finish_plane())
     finish_out(NUM_STEPS)
     alpha, beta = finish_line(par)
     ab_ref[0, NUM_STEPS - 1] = alpha[0, 0]
     ab_ref[1, NUM_STEPS - 1] = beta[0, 0]
     own_rows(NUM_STEPS, alpha, beta_prev, beta)
+    drain_sums(par)
+
+
+def end_kernel(vec_ref, ab_ref, vec_out, alpha_out, beta_out):
+    vec_out[...] = vec_ref[...]
+    for k in range(NUM_STEPS):
+        alpha_out[k] = ab_ref[0, k]
+        beta_out[k] = ab_ref[1, k]
 
 
 def vmem(n):
@@ -528,8 +559,16 @@
             op_pair.transpose(1, 2, 0),
             right_env,
         )
+        short = jax.ShapeDtypeStruct((NUM_STEPS,), F32)
+        vecs, alpha, beta = pl.pallas_call(
+            end_kernel,
+            out_shape=(jax.ShapeDtypeStruct(vecs.shape, F32), short, short),
+            in_specs=vmem(1) + [smem],
+            out_specs=(vmem(1)[0], smem, smem),
+            name="result",
+        )(vecs, ab)
         vecs = vecs.reshape(nv, 3, 3, rows, right_dim).transpose(0, 3, 1, 2, 4)
-        return vecs, ab[0], ab[1]
+        return vecs, alpha, beta
 
     return jax.shard_map(
         local_run,

time: 162 us -> 161 us (level)
  local copies, waits for them, and re-layouts: 2.92 us -> 0 us
  Pallas kernels: 158 us -> 160 us
    pallas_call x0 -> x1, Pallas kernels: none -> 1.69 us  [local_run(): pl.pallas_call(end_kernel, out_shape=(jax.ShapeDtypeStruct(vecs.shape, F3...]
    unnamed x1 -> x0, local copies, waits for them, and re-layouts: 1.66 us -> none
where the time goes in v7:
time: 161 us
  Pallas kernels  160 us (99%)
    pallas_call x1, Pallas kernels, local_run(): pl.pallas_call(functools.partial(main_kernel, nz, float(count)), out_shap...  159 us

profile of v7, /device:TPU:1, one launch (start us, length us, event | category | flops | bytes accessed | tf_op | source)
XLA Modules:
  0.0 160.9 jit_solution(14871228210989676924)
XLA Ops:
  0.6 158.6 %lanczos.1 = (f32[7,9,2,512]{3,2,1,0:T(2,128)}, f32[2,6]{1,0:T(2,128)}) custom-call(f32[9,2,512]{2,1,0:T(2,128)} %bitcast.7, bf16[32,2,512]{2,1,0:T(2,128)(2,1)} %left_ref.1, bf16[9,9,32]{2,1,0:T(8,128)(2,1)} %bitcast.8, bf16[32,512,512]{2,1,0:T(8,128)(2,1)} %right_ref.1), custom_call_target="tpu_custom_call" | custom-call | tf_op jit(solution)/shard_map/lanczos/pallas_call | solution.py:518
  159.2 1.7 %result.1 = (f32[7,9,2,512]{3,2,1,0:T(2,128)}, f32[6]{0:T(128)}, f32[6]{0:T(128)}) custom-call(f32[7,9,2,512]{3,2,1,0:T(2,128)} %get-tuple-element.8.vec_ref, f32[2,6]{1,0:T(2,128)} %get-tuple-element.9.ab_ref), custom_call_target="tpu_custom_call" | custom-call | tf_op jit(solution)/shard_map/result/pallas_call | solution.py:563
